TPU v7x, 512 devices: a whole 4x8x8 slice. The times are simulated.
512 devices in a mesh: wide: 32 (over z_lo, y), narrow: 16 (over z_hi, x, core).
Axes of the slice: x: 4, y: 8, z: 8 (z_hi: 2, z_lo: 4; z = z_hi * 4 + z_lo), core: 2. Of those that a mesh axis runs over, the one named last changes fastest.
Arguments:
- stored_features: bfloat16 [64, 64, 64, 128], P(None, 'wide', 'narrow'), may hold values from -127 to 127
- channel_scale: float32 [64], replicated, may hold values from 0.005 to 0.05
- channel_shift: float32 [64], replicated, may hold values from -0.5 to 0.5
- first_weight: bfloat16 [64, 1728], replicated, may hold values from -0.21875 to 0.21875
- second_weight: bfloat16 [128, 1728], replicated, may hold values from -0.21875 to 0.21875
- third_weight: bfloat16 [256, 3456], P('narrow'), may hold values from -0.15625 to 0.15625
Outputs:
- coarse_features: bfloat16 [256, 32, 2048], P('narrow', 'wide')
All inputs are finite; a program needn't handle non-finite values.
Results may differ from a plain program's by a relative error of at most 0.0057.
Values may be sent and summed in bfloat16 or wider, within the bound.
A program may use at most 64 MiB of HBM per device.

v0:
```python
import jax
import jax.numpy as jnp
from jax import lax
from jax.sharding import PartitionSpec as P


def with_halo(block, sides, width):
    for axis, dim in sides:
        count = lax.axis_size(axis)
        forward = [(i, i + 1) for i in range(count - 1)]
        backward = [(target, source) for source, target in forward]
        low = lax.ppermute(
            lax.slice_in_dim(block, block.shape[dim] - width, None, axis=dim), axis, forward
        )
        high = lax.ppermute(lax.slice_in_dim(block, 0, width, axis=dim), axis, backward)
        block = jnp.concatenate([low, block, high], axis=dim)
    return block


def convolve(padded, weight, depth_rows, height_rows):
    channels = padded.shape[0]
    width_cells = padded.shape[3]
    padded_width = jnp.pad(padded, ((0, 0), (0, 0), (0, 0), (1, 1)))
    accumulated = None
    for depth_off in range(3):
        for height_off in range(3):
            stacked = jnp.concatenate(
                [
                    padded_width[
                        :,
                        depth_off : depth_off + depth_rows,
                        height_off : height_off + height_rows,
                        width_off : width_off + width_cells,
                    ]
                    for width_off in range(3)
                ],
                axis=0,
            )
            stacked = stacked.reshape(3 * channels, -1)
            column_start = (depth_off * 3 + height_off) * 3 * channels
            weight_block = weight[:, column_start : column_start + 3 * channels]
            product = jnp.dot(weight_block, stacked, preferred_element_type=jnp.float32)
            accumulated = product if accumulated is None else accumulated + product
    return accumulated.reshape(weight.shape[0], depth_rows, height_rows, width_cells)


def body(stored_features, channel_scale, channel_shift, first_weight, second_weight, third_weight):
    depth_rows = stored_features.shape[1]
    height_rows = stored_features.shape[2]
    features = (
        stored_features.astype(jnp.float32) * channel_scale[:, None, None, None]
        + channel_shift[:, None, None, None]
    ).astype(jnp.bfloat16)
    padded = with_halo(features, (("wide", 1), ("narrow", 2)), 1)
    first_hidden = jnp.maximum(convolve(padded, first_weight, depth_rows, height_rows), 0.0).astype(
        jnp.bfloat16
    )
    padded_hidden = with_halo(first_hidden, (("wide", 1), ("narrow", 2)), 1)
    second_hidden = jnp.maximum(
        convolve(padded_hidden, second_weight, depth_rows, height_rows), 0.0
    ).astype(jnp.bfloat16)
    channels, _, _, width_cells = second_hidden.shape
    pooled = second_hidden.reshape(
        channels, depth_rows // 2, 2, height_rows // 2, 2, width_cells // 2, 2
    ).max(axis=(2, 4, 6))
    whole_height = lax.all_gather(pooled, "narrow", axis=2, tiled=True)
    slab = with_halo(whole_height, (("wide", 1),), 1)
    slab = jnp.pad(slab, ((0, 0), (0, 0), (1, 1), (0, 0)))
    coarse = jnp.maximum(
        convolve(slab, third_weight, depth_rows // 2, whole_height.shape[2]), 0.0
    ).astype(jnp.bfloat16)
    return coarse.reshape(coarse.shape[0], coarse.shape[1], -1)


def solution(mesh):
    in_specs = (P(None, "wide", "narrow", None), P(), P(), P(), P(), P("narrow", None))
    out_specs = P("narrow", "wide", None)
    return jax.shard_map(body, mesh=mesh, in_specs=in_specs, out_specs=out_specs, check_vma=False)
```

profile of v0, /device:TPU:450, one launch (start us, length us, event | category | flops | bytes accessed | tf_op | source)
XLA Modules:
  0.0 157.6 jit_solution(7910637363971819520)
XLA Ops:
  1.2 3.5 %collective-permute-start = (bf16[64,1,4,128]{3,2,1,0:T(4,128)(2,1)S(1)}, bf16[64,1,4,128]{3,2,1,0:T(4,128)(2,1)S(1)}, u32[]{:S(2)}, u32[]{:S(2)}) collective-permute-start(bf16[64,1,4,128]{3,2,1,0:T(4,128)(2,1)S(1)} %get-tuple-element.89), channel_id=1, source_target_pairs={{0,16},{16,32},{32,48},{48,64},{64,80},{80,96},{96,112},{112,128},... | collective-permute-start | bytes 196616 | tf_op jit(solution)/shard_map/ppermute | solution.py:12
  4.7 4.5 %collective-permute-start.1 = (bf16[64,1,4,128]{3,2,1,0:T(4,128)(2,1)S(1)}, bf16[64,1,4,128]{3,2,1,0:T(4,128)(2,1)S(1)}, u32[]{:S(2)}, u32[]{:S(2)}) collective-permute-start(bf16[64,1,4,128]{3,2,1,0:T(4,128)(2,1)S(1)} %get-tuple-element.90), channel_id=1, source_target_pairs={{16,0},{32,16},{48,32},{64,48},{80,64},{96,80},{112,96},{128,112},... | collective-permute-start | bytes 196616 | tf_op jit(solution)/shard_map/ppermute | solution.py:15
  11.4 1.9 %collective-permute-start.3 = (bf16[64,4,1,128]{3,2,1,0:T(2,128)(2,1)S(1)}, bf16[64,4,1,128]{3,2,1,0:T(2,128)(2,1)S(1)}, u32[]{:S(2)}, u32[]{:S(2)}) collective-permute-start(bf16[64,4,1,128]{3,2,1,0:T(2,128)(2,1)S(1)} %get-tuple-element.79), channel_id=1, source_target_pairs={{1,0},{2,1},{3,2},{4,3},{5,4},{6,5},{7,6},{8,7},{9,8},{10,9},{11,1... | collective-permute-start | bytes 196616 | tf_op jit(solution)/shard_map/ppermute | solution.py:15
  13.4 2.4 %collective-permute-start.2 = (bf16[64,4,1,128]{3,2,1,0:T(2,128)(2,1)S(1)}, bf16[64,4,1,128]{3,2,1,0:T(2,128)(2,1)S(1)}, u32[]{:S(2)}, u32[]{:S(2)}) collective-permute-start(bf16[64,4,1,128]{3,2,1,0:T(2,128)(2,1)S(1)} %get-tuple-element.80), channel_id=1, source_target_pairs={{0,1},{1,2},{2,3},{3,4},{4,5},{5,6},{6,7},{7,8},{8,9},{9,10},{10,1... | collective-permute-start | bytes 196616 | tf_op jit(solution)/shard_map/ppermute | solution.py:12
  15.9 3.8 %collective-permute-done.2 = bf16[64,4,1,128]{3,2,1,0:T(2,128)(2,1)S(1)} collective-permute-done((bf16[64,4,1,128]{3,2,1,0:T(2,128)(2,1)S(1)}, bf16[64,4,1,128]{3,2,1,0:T(2,128)(2,1)S(1)}, u32[]{:S(2)}, u32[]{:S(2)}) %collective-permute-start.2) | collective-permute-done | bytes 65568 | tf_op jit(solution)/shard_map/ppermute | solution.py:12
  19.7 1.8 %fusion.21 = bf16[64,4,6,130]{3,2,1,0:T(8,128)(2,1)S(1)} fusion(bf16[64,4,1,128]{3,2,1,0:T(2,128)(2,1)S(1)} %collective-permute-done.3, bf16[64,4,1,128]{3,2,1,0:T(2,128)(2,1)S(1)} %collective-permute-done.2, bf16[64,1,4,128]{3,2,1,0:T(4,128)(2,1)S(1)} %collective-permute-done.1, bf16[64,2,4,128]{3,2,1,0:T(4,128)(2,1)S(1)} %add_convert_fusion, ...), kind=kLoop, calls=%fused_computation.60 | loop fusion | flops 3594240 | bytes 792576 | tf_op jit(solution)/shard_map/concatenate | solution.py:16
  21.4 2.3 %fusion.89 = (bf16[64,2,4,128]{3,2,1,0:T(4,128)(2,1)S(1)}, bf16[64,2,4,128]{3,2,1,0:T(4,128)(2,1)S(1)}, bf16[64,2,4,128]{3,2,1,0:T(4,128)(2,1)}, bf16[64,2,4,128...) fusion(bf16[64,4,6,130]{3,2,1,0:T(8,128)(2,1)S(1)} %fusion.21), kind=kLoop, calls=%fused_computation.181 | loop fusion | bytes 4718592 | tf_op jit(solution)/shard_map/slice | solution.py:29
  26.3 2.4 %fusion.45 = (bf16[192,2,4,128]{3,2,1,0:T(4,128)(2,1)S(1)}, bf16[192,2,4,128]{3,2,1,0:T(4,128)(2,1)S(1)}, bf16[192,2,4,128]{3,2,1,0:T(4,128)(2,1)S(1)}) fusion(bf16[64,4,1,128]{3,2,1,0:T(2,128)(2,1)S(1)} %collective-permute-done.2, bf16[64,1,4,128]{3,2,1,0:T(4,128)(2,1)S(1)} %collective-permute-done.1, bf16[64,2,4,128]{3,2,1,0:T(4,128)(2,1)S(1)} %add_convert_fusion, ...), kind=kLoop, calls=%fused_computation.97 | loop fusion | flops 7077888 | bytes 2293760 | tf_op jit(solution)/shard_map/concatenate | solution.py:27
  29.0 2.9 %fusion.43 = (bf16[192,2,4,128]{3,2,1,0:T(4,128)(2,1)}, bf16[192,2,4,128]{3,2,1,0:T(4,128)(2,1)S(1)}, bf16[192,2,4,128]{3,2,1,0:T(4,128)(2,1)}) fusion(bf16[64,1,4,128]{3,2,1,0:T(4,128)(2,1)S(1)} %collective-permute-done.1, bf16[64,2,4,128]{3,2,1,0:T(4,128)(2,1)S(1)} %add_convert_fusion, bf16[64,2,4,128]{3,2,1,0:T(4,128)(2,1)S(1)} %get-tuple-element.48, ...), kind=kLoop, calls=%fused_computation.94 | loop fusion | flops 1572864 | bytes 2228224 | tf_op jit(solution)/shard_map/concatenate | solution.py:27
  42.4 3.3 %collective-permute-start.4 = (bf16[64,1,4,128]{3,2,1,0:T(4,128)(2,1)S(1)}, bf16[64,1,4,128]{3,2,1,0:T(4,128)(2,1)S(1)}, u32[]{:S(2)}, u32[]{:S(2)}) collective-permute-start(bf16[64,1,4,128]{3,2,1,0:T(4,128)(2,1)S(1)} %get-tuple-element.85), channel_id=1, source_target_pairs={{0,16},{16,32},{32,48},{48,64},{64,80},{80,96},{96,112},{112,128},... | collective-permute-start | bytes 196616 | tf_op jit(solution)/shard_map/ppermute | solution.py:12
  45.7 5.0 %collective-permute-start.5 = (bf16[64,1,4,128]{3,2,1,0:T(4,128)(2,1)S(1)}, bf16[64,1,4,128]{3,2,1,0:T(4,128)(2,1)S(1)}, u32[]{:S(2)}, u32[]{:S(2)}) collective-permute-start(bf16[64,1,4,128]{3,2,1,0:T(4,128)(2,1)S(1)} %get-tuple-element.84), channel_id=1, source_target_pairs={{16,0},{32,16},{48,32},{64,48},{80,64},{96,80},{112,96},{128,112},... | collective-permute-start | bytes 196616 | tf_op jit(solution)/shard_map/ppermute | solution.py:15
  52.8 1.9 %collective-permute-start.7 = (bf16[64,4,1,128]{3,2,1,0:T(2,128)(2,1)S(1)}, bf16[64,4,1,128]{3,2,1,0:T(2,128)(2,1)S(1)}, u32[]{:S(2)}, u32[]{:S(2)}) collective-permute-start(bf16[64,4,1,128]{3,2,1,0:T(2,128)(2,1)S(1)} %get-tuple-element.77), channel_id=1, source_target_pairs={{1,0},{2,1},{3,2},{4,3},{5,4},{6,5},{7,6},{8,7},{9,8},{10,9},{11,1... | collective-permute-start | bytes 196616 | tf_op jit(solution)/shard_map/ppermute | solution.py:15
  54.8 2.6 %collective-permute-start.6 = (bf16[64,4,1,128]{3,2,1,0:T(2,128)(2,1)S(1)}, bf16[64,4,1,128]{3,2,1,0:T(2,128)(2,1)S(1)}, u32[]{:S(2)}, u32[]{:S(2)}) collective-permute-start(bf16[64,4,1,128]{3,2,1,0:T(2,128)(2,1)S(1)} %get-tuple-element.78), channel_id=1, source_target_pairs={{0,1},{1,2},{2,3},{3,4},{4,5},{5,6},{6,7},{7,8},{8,9},{9,10},{10,1... | collective-permute-start | bytes 196616 | tf_op jit(solution)/shard_map/ppermute | solution.py:12
  57.4 10.0 %collective-permute-done.6 = bf16[64,4,1,128]{3,2,1,0:T(2,128)(2,1)S(1)} collective-permute-done((bf16[64,4,1,128]{3,2,1,0:T(2,128)(2,1)S(1)}, bf16[64,4,1,128]{3,2,1,0:T(2,128)(2,1)S(1)}, u32[]{:S(2)}, u32[]{:S(2)}) %collective-permute-start.6) | collective-permute-done | bytes 65568 | tf_op jit(solution)/shard_map/ppermute | solution.py:12
  68.7 2.3 %fusion.88 = (bf16[64,2,4,128]{3,2,1,0:T(4,128)(2,1)S(1)}, bf16[64,2,4,128]{3,2,1,0:T(4,128)(2,1)S(1)}, bf16[64,2,4,128]{3,2,1,0:T(4,128)(2,1)S(1)}, bf16[64,2,4...) fusion(bf16[64,4,6,130]{3,2,1,0:T(8,128)(2,1)S(1)} %select_maxi, ...), kind=kLoop, calls=%fused_computation.180 | loop fusion | bytes 4718592 | tf_op jit(solution)/shard_map/slice | solution.py:29
  72.1 1.9 %fusion.29 = (bf16[192,2,4,128]{3,2,1,0:T(4,128)(2,1)S(1)}, bf16[192,2,4,128]{3,2,1,0:T(4,128)(2,1)S(1)}, bf16[192,2,4,128]{3,2,1,0:T(4,128)(2,1)S(1)}) fusion(bf16[64,4,4,128]{3,2,1,0:T(4,128)(2,1)S(1)} %constant_dynamic-update-slice_fusion, bf16[64,4,1,128]{3,2,1,0:T(2,128)(2,1)S(1)} %collective-permute-done.6, ...), kind=kLoop, calls=%fused_computation.71 | loop fusion | flops 4718592 | bytes 2293760 | tf_op jit(solution)/shard_map/concatenate | solution.py:27
  75.4 2.9 %fusion.27 = (bf16[192,2,4,128]{3,2,1,0:T(4,128)(2,1)S(1)}, bf16[192,2,4,128]{3,2,1,0:T(4,128)(2,1)}, bf16[192,2,4,128]{3,2,1,0:T(4,128)(2,1)}) fusion(bf16[64,1,4,128]{3,2,1,0:T(4,128)(2,1)} %copy-done.5, bf16[64,2,4,128]{3,2,1,0:T(4,128)(2,1)S(1)} %convert_element_type.44, bf16[64,2,4,128]{3,2,1,0:T(4,128)(2,1)S(1)} %get-tuple-element.30, ...), kind=kLoop, calls=%fused_computation.68 | loop fusion | flops 1572864 | bytes 2228224 | tf_op jit(solution)/shard_map/concatenate | solution.py:27
  79.8 2.0 %reshape.126 = bf16[192,1024]{1,0:T(8,128)(2,1)} reshape(bf16[192,2,4,128]{3,2,1,0:T(4,128)(2,1)} %get-tuple-element.83) | data formatting | bytes 786432 | tf_op jit(solution)/shard_map/reshape | solution.py:39
  87.3 32.8 %all-gather = bf16[128,32,64]{0,2,1:T(8,128)(2,1)S(1)} all-gather(bf16[128,2,64]{0,2,1:T(8,128)(2,1)S(1)} %reduce_max.11), channel_id=2, replica_groups=mesh['wide'=32,'narrow'=16] {'narrow'}, dimensions={1}, use_global_device_ids=true | all-gather | bytes 557056 | tf_op jit(solution)/shard_map/all_gather | solution.py:66
  120.2 6.7 %collective-permute-start.9 = (bf16[128,1,32,64]{0,3,2,1:T(8,128)(2,1)S(1)}, bf16[128,1,32,64]{0,3,2,1:T(8,128)(2,1)S(1)}, u32[]{:S(2)}, u32[]{:S(2)}) collective-permute-start(bf16[128,1,32,64]{0,3,2,1:T(8,128)(2,1)S(1)} %bitcast.55), channel_id=1, source_target_pairs={{16,0},{32,16},{48,32},{64,48},{80,64},{96,80},{112,96},{128,112},... | collective-permute-start | bytes 1572872 | tf_op jit(solution)/shard_map/ppermute | solution.py:15
  126.9 2.1 %collective-permute-start.8 = (bf16[128,1,32,64]{0,3,2,1:T(8,128)(2,1)S(1)}, bf16[128,1,32,64]{0,3,2,1:T(8,128)(2,1)S(1)}, u32[]{:S(2)}, u32[]{:S(2)}) collective-permute-start(bf16[128,1,32,64]{0,3,2,1:T(8,128)(2,1)S(1)} %bitcast.56), channel_id=1, source_target_pairs={{0,16},{16,32},{32,48},{48,64},{64,80},{80,96},{96,112},{112,128},... | collective-permute-start | bytes 1572872 | tf_op jit(solution)/shard_map/ppermute | solution.py:12
  129.0 9.5 %collective-permute-done.9 = bf16[128,1,32,64]{0,3,2,1:T(8,128)(2,1)S(1)} collective-permute-done((bf16[128,1,32,64]{0,3,2,1:T(8,128)(2,1)S(1)}, bf16[128,1,32,64]{0,3,2,1:T(8,128)(2,1)S(1)}, u32[]{:S(2)}, u32[]{:S(2)}) %collective-permute-start.9) | collective-permute-done | bytes 524320 | tf_op jit(solution)/shard_map/ppermute | solution.py:15
  138.5 6.2 %collective-permute-done.8 = bf16[128,1,32,64]{0,3,2,1:T(8,128)(2,1)S(1)} collective-permute-done((bf16[128,1,32,64]{0,3,2,1:T(8,128)(2,1)S(1)}, bf16[128,1,32,64]{0,3,2,1:T(8,128)(2,1)S(1)}, u32[]{:S(2)}, u32[]{:S(2)}) %collective-permute-start.8) | collective-permute-done | bytes 524320 | tf_op jit(solution)/shard_map/ppermute | solution.py:12
  147.0 2.6 %fusion.86 = (bf16[128,1,32,64]{0,3,2,1:T(8,128)(2,1)S(1)}, bf16[128,1,32,64]{0,3,2,1:T(8,128)(2,1)S(1)}, bf16[128,1,32,64]{0,3,2,1:T(8,128)(2,1)S(1)}, bf16[128...) fusion(bf16[128,3,34,64]{0,3,2,1:T(8,128)(2,1)S(1)} %fusion.9), kind=kLoop, calls=%fused_computation.178 | loop fusion | bytes 9011200 | tf_op jit(solution)/shard_map/slice | solution.py:29
  (86 shorter events, 39.7 us)
Async XLA Ops:
  1.2 8.3 %collective-permute-start = (bf16[64,1,4,128]{3,2,1,0:T(4,128)(2,1)S(1)}, bf16[64,1,4,128]{3,2,1,0:T(4,128)(2,1)S(1)}, u32[]{:S(2)}, u32[]{:S(2)}) collective-permute-start(bf16[64,1,4,128]{3,2,1,0:T(4,128)(2,1)S(1)} %get-tuple-element.89), channel_id=1, source_target_pairs={{0,16},{16,32},{32,48},{48,64},{64,80},{80,96},{96,112},{112,128},... | collective-permute-start | bytes 196616 | tf_op jit(solution)/shard_map/ppermute | solution.py:12
  4.7 6.4 %collective-permute-start.1 = (bf16[64,1,4,128]{3,2,1,0:T(4,128)(2,1)S(1)}, bf16[64,1,4,128]{3,2,1,0:T(4,128)(2,1)S(1)}, u32[]{:S(2)}, u32[]{:S(2)}) collective-permute-start(bf16[64,1,4,128]{3,2,1,0:T(4,128)(2,1)S(1)} %get-tuple-element.90), channel_id=1, source_target_pairs={{16,0},{32,16},{48,32},{64,48},{80,64},{96,80},{112,96},{128,112},... | collective-permute-start | bytes 196616 | tf_op jit(solution)/shard_map/ppermute | solution.py:15
  11.4 4.4 %collective-permute-start.3 = (bf16[64,4,1,128]{3,2,1,0:T(2,128)(2,1)S(1)}, bf16[64,4,1,128]{3,2,1,0:T(2,128)(2,1)S(1)}, u32[]{:S(2)}, u32[]{:S(2)}) collective-permute-start(bf16[64,4,1,128]{3,2,1,0:T(2,128)(2,1)S(1)} %get-tuple-element.79), channel_id=1, source_target_pairs={{1,0},{2,1},{3,2},{4,3},{5,4},{6,5},{7,6},{8,7},{9,8},{10,9},{11,1... | collective-permute-start | bytes 196616 | tf_op jit(solution)/shard_map/ppermute | solution.py:15
  13.4 6.3 %collective-permute-start.2 = (bf16[64,4,1,128]{3,2,1,0:T(2,128)(2,1)S(1)}, bf16[64,4,1,128]{3,2,1,0:T(2,128)(2,1)S(1)}, u32[]{:S(2)}, u32[]{:S(2)}) collective-permute-start(bf16[64,4,1,128]{3,2,1,0:T(2,128)(2,1)S(1)} %get-tuple-element.80), channel_id=1, source_target_pairs={{0,1},{1,2},{2,3},{3,4},{4,5},{5,6},{6,7},{7,8},{8,9},{9,10},{10,1... | collective-permute-start | bytes 196616 | tf_op jit(solution)/shard_map/ppermute | solution.py:12
  25.4 0.9 copy-start.1
  33.2 4.4 %copy-start.3 = (bf16[64,1728]{1,0:T(8,128)(2,1)S(1)}, bf16[64,1728]{1,0:T(8,128)(2,1)}, u32[]{:S(2)}) copy-start(bf16[64,1728]{1,0:T(8,128)(2,1)} %param.9) | copy-start | bytes 663556
  36.5 3.7 %copy-start = (bf16[192,1024]{1,0:T(8,128)(2,1)S(1)}, bf16[192,1024]{1,0:T(8,128)(2,1)}, u32[]{:S(2)}) copy-start(bf16[192,1024]{1,0:T(8,128)(2,1)} %reshape.119) | copy-start | bytes 1179652
  42.4 8.6 %collective-permute-start.4 = (bf16[64,1,4,128]{3,2,1,0:T(4,128)(2,1)S(1)}, bf16[64,1,4,128]{3,2,1,0:T(4,128)(2,1)S(1)}, u32[]{:S(2)}, u32[]{:S(2)}) collective-permute-start(bf16[64,1,4,128]{3,2,1,0:T(4,128)(2,1)S(1)} %get-tuple-element.85), channel_id=1, source_target_pairs={{0,16},{16,32},{32,48},{48,64},{64,80},{80,96},{96,112},{112,128},... | collective-permute-start | bytes 196616 | tf_op jit(solution)/shard_map/ppermute | solution.py:12
  45.7 6.9 %collective-permute-start.5 = (bf16[64,1,4,128]{3,2,1,0:T(4,128)(2,1)S(1)}, bf16[64,1,4,128]{3,2,1,0:T(4,128)(2,1)S(1)}, u32[]{:S(2)}, u32[]{:S(2)}) collective-permute-start(bf16[64,1,4,128]{3,2,1,0:T(4,128)(2,1)S(1)} %get-tuple-element.84), channel_id=1, source_target_pairs={{16,0},{32,16},{48,32},{64,48},{80,64},{96,80},{112,96},{128,112},... | collective-permute-start | bytes 196616 | tf_op jit(solution)/shard_map/ppermute | solution.py:15
  51.0 16.4 %copy-start.4 = (bf16[64,1,4,128]{3,2,1,0:T(4,128)(2,1)}, bf16[64,1,4,128]{3,2,1,0:T(4,128)(2,1)S(1)}, u32[]{:S(2)}) copy-start(bf16[64,1,4,128]{3,2,1,0:T(4,128)(2,1)S(1)} %collective-permute-done.4) | copy-start | bytes 196612
  52.6 14.8 %copy-start.5 = (bf16[64,1,4,128]{3,2,1,0:T(4,128)(2,1)}, bf16[64,1,4,128]{3,2,1,0:T(4,128)(2,1)S(1)}, u32[]{:S(2)}) copy-start(bf16[64,1,4,128]{3,2,1,0:T(4,128)(2,1)S(1)} %collective-permute-done.5) | copy-start | bytes 196612
  52.8 4.5 %collective-permute-start.7 = (bf16[64,4,1,128]{3,2,1,0:T(2,128)(2,1)S(1)}, bf16[64,4,1,128]{3,2,1,0:T(2,128)(2,1)S(1)}, u32[]{:S(2)}, u32[]{:S(2)}) collective-permute-start(bf16[64,4,1,128]{3,2,1,0:T(2,128)(2,1)S(1)} %get-tuple-element.77), channel_id=1, source_target_pairs={{1,0},{2,1},{3,2},{4,3},{5,4},{6,5},{7,6},{8,7},{9,8},{10,9},{11,1... | collective-permute-start | bytes 196616 | tf_op jit(solution)/shard_map/ppermute | solution.py:15
  54.8 12.6 %collective-permute-start.6 = (bf16[64,4,1,128]{3,2,1,0:T(2,128)(2,1)S(1)}, bf16[64,4,1,128]{3,2,1,0:T(2,128)(2,1)S(1)}, u32[]{:S(2)}, u32[]{:S(2)}) collective-permute-start(bf16[64,4,1,128]{3,2,1,0:T(2,128)(2,1)S(1)} %get-tuple-element.78), channel_id=1, source_target_pairs={{0,1},{1,2},{2,3},{3,4},{4,5},{5,6},{6,7},{7,8},{8,9},{9,10},{10,1... | collective-permute-start | bytes 196616 | tf_op jit(solution)/shard_map/ppermute | solution.py:12
  81.9 2.6 %copy-start.2 = (bf16[128,1728]{0,1:T(8,128)(2,1)S(1)}, bf16[128,1728]{0,1:T(8,128)(2,1)}, u32[]{:S(2)}) copy-start(bf16[128,1728]{0,1:T(8,128)(2,1)} %param.10) | copy-start | bytes 1327108
  120.2 18.4 %collective-permute-start.9 = (bf16[128,1,32,64]{0,3,2,1:T(8,128)(2,1)S(1)}, bf16[128,1,32,64]{0,3,2,1:T(8,128)(2,1)S(1)}, u32[]{:S(2)}, u32[]{:S(2)}) collective-permute-start(bf16[128,1,32,64]{0,3,2,1:T(8,128)(2,1)S(1)} %bitcast.55), channel_id=1, source_target_pairs={{16,0},{32,16},{48,32},{64,48},{80,64},{96,80},{112,96},{128,112},... | collective-permute-start | bytes 1572872 | tf_op jit(solution)/shard_map/ppermute | solution.py:15
  126.9 17.9 %collective-permute-start.8 = (bf16[128,1,32,64]{0,3,2,1:T(8,128)(2,1)S(1)}, bf16[128,1,32,64]{0,3,2,1:T(8,128)(2,1)S(1)}, u32[]{:S(2)}, u32[]{:S(2)}) collective-permute-start(bf16[128,1,32,64]{0,3,2,1:T(8,128)(2,1)S(1)} %bitcast.56), channel_id=1, source_target_pairs={{0,16},{16,32},{32,48},{48,64},{64,80},{80,96},{96,112},{112,128},... | collective-permute-start | bytes 1572872 | tf_op jit(solution)/shard_map/ppermute | solution.py:12
  149.7 0.9 copy-start.6
where the time goes:
time: 158 us
  starting transfers between devices  33.9 us (21%)
  waiting for transfers between devices  33.3 us (21%)
  blocking collectives  32.8 us (21%)
  local copies, waits for them, and re-layouts  22.3 us (14%)
  other arithmetic  19.8 us (13%)
  matrix products  15 us (9%)
    all_gather x1, blocking collectives, body(): whole_height = lax.all_gather(pooled, 'narrow', axis=2, tiled=True)  32.8 us
    ppermute x5, waiting for transfers between devices, with_halo(): lax.ppermute(lax.slice_in_dim(block, block.shape[dim] - width, None, axis...  20.6 us
    ppermute x5, starting transfers between devices, with_halo(): lax.ppermute(lax.slice_in_dim(block, 0, width, axis=dim), axis, backward)  20 us
    dot_general x27, matrix products, convolve(): product = jnp.dot(weight_block, stacked, preferred_element_type=jnp.float32)  15 us
    concatenate x11, other arithmetic, convolve(): jnp.concatenate([padded_width[:, depth_off:depth_off + depth_rows, height...  14.8 us
    ppermute x5, starting transfers between devices, with_halo(): lax.ppermute(lax.slice_in_dim(block, block.shape[dim] - width, None, axis...  13.9 us
    ppermute x5, waiting for transfers between devices, with_halo(): lax.ppermute(lax.slice_in_dim(block, 0, width, axis=dim), axis, backward)  12.7 us
    reshape x18, local copies, waits for them, and re-layouts, convolve(): stacked = stacked.reshape(3 * channels, -1)  11.8 us
  transfers between devices with their start and end apart: 10, of which 9 were waited for; matrix products, arithmetic and copies ran while one was open for 0% of the time, Pallas kernels for 0%

commit v1 on v0

v1 whole, which is shorter than its diff:
```python
import functools

import jax
import jax.numpy as jnp
from jax import lax
from jax.experimental import pallas as pl
from jax.experimental.pallas import tpu as pltpu
from jax.sharding import PartitionSpec as P

BF = jnp.bfloat16
F32 = jnp.float32
MESH = pl.DeviceIdType.MESH

H0, D0, G0, P0, WX0, WZ0, WF0, WC0, A0 = 0, 2, 4, 8, 16, 19, 20, 23, 31
NSEM = A0 + 16


def kernel(nw, nn, x_ref, sc_ref, sh_ref, w1_ref, w2_ref, w3_ref, out_ref,
           xf, fb, xs1, xs2, w1p, w2p, pb, xs3, w3g, ob, ssem, rsem):
    w = lax.axis_index("wide")
    n = lax.axis_index("narrow")
    half = nn // 2
    zh = n // half
    within = n % half
    mate = n + 1 - 2 * (n % 2)
    zmate = (n + half) % nn

    def xmate(k):
        return zh * half + (within + 2 * k) % half

    def side(i):
        return i - 1

    wok = [w > 0, None, w < nw - 1]
    nok = [n > 0, None, n < nn - 1]

    def ok(i, j):
        if i == 1:
            return nok[j]
        if j == 1:
            return wok[i]
        return jnp.logical_and(wok[i], nok[j])

    near = [(i, j) for i in range(3) for j in range(3) if (i, j) != (1, 1)]

    barrier = pltpu.get_barrier_semaphore()
    for k in range(1, nn):
        pl.semaphore_signal(barrier, inc=1, device_id=(w, (n + k) % nn), device_id_type=MESH)
    for i in (0, 2):
        for j in range(3):
            @pl.when(ok(i, j))
            def _():
                pl.semaphore_signal(
                    barrier, inc=1, device_id=(w + side(i), n + side(j)), device_id_type=MESH
                )

    one = jnp.int32(1)
    zero = jnp.int32(0)
    wcount = jnp.where(w > 0, one, zero) + jnp.where(w < nw - 1, one, zero)
    ncount = jnp.where(n > 0, one, zero) + jnp.where(n < nn - 1, one, zero)
    expected = (nn - 1) + wcount * (1 + ncount)

    @pl.when(n == 0)
    def _():
        fb[:, :, 0:256] = jnp.zeros((6, 64, 256), BF)
        pb[:, 0] = jnp.zeros((3, 128, 128), BF)

    @pl.when(n == nn - 1)
    def _():
        fb[:, :, 768:1024] = jnp.zeros((6, 64, 256), BF)
        pb[:, 2] = jnp.zeros((3, 128, 128), BF)

    @pl.when(w == 0)
    def _():
        fb[0:2] = jnp.zeros((2, 64, 1024), BF)
        pb[0] = jnp.zeros((3, 128, 128), BF)

    @pl.when(w == nw - 1)
    def _():
        fb[4:6] = jnp.zeros((2, 64, 1024), BF)
        pb[2] = jnp.zeros((3, 128, 128), BF)

    lane = lax.broadcasted_iota(jnp.int32, (1, 128), 1)

    def shifted(t, period):
        pos = lane % period
        before = jnp.where(pos > 0, pltpu.roll(t, 1, 1), 0.0)
        after = jnp.where(pos < period - 1, pltpu.roll(t, 127, 1), 0.0)
        return before.astype(BF), t.astype(BF), after.astype(BF)

    def stack1(d, h):
        t = fb[d, :, h * 128:(h + 1) * 128].astype(F32)
        for e, v in enumerate(shifted(t, 128)):
            xs1[d * 192 + e * 64:d * 192 + (e + 1) * 64, h * 128:(h + 1) * 128] = v

    eye = lax.broadcasted_iota(jnp.int32, (64, 64), 0) == lax.broadcasted_iota(jnp.int32, (64, 64), 1)

    def column(ref):
        return jnp.sum(jnp.where(eye, ref[...], 0.0), axis=1, keepdims=True)

    scale = column(sc_ref)
    shift = column(sh_ref)
    xf[...] = x_ref[...].astype(F32)
    for d in range(2):
        for h in range(4):
            t = xf[pl.ds(d * 4 + h, 64, stride=8), :]
            fb[2 + d, :, (2 + h) * 128:(3 + h) * 128] = (t * scale + shift).astype(BF)

    for a in range(3):
        for b in range(3):
            c0 = (a * 3 + b) * 192
            w1p[b * 64:(b + 1) * 64, a * 192:(a + 1) * 192] = w1_ref[:, c0:c0 + 192]
            w2p[b * 128:(b + 1) * 128, a * 192:(a + 1) * 192] = w2_ref[:, c0:c0 + 192]
    w3g[pl.ds(pl.multiple_of(n * 16, 16), 16), :] = w3_ref[...]

    pl.semaphore_wait(barrier, expected)

    def remote(src, dst, s, dev, r=None):
        return pltpu.make_async_remote_copy(
            src_ref=src, dst_ref=dst, send_sem=ssem.at[s], recv_sem=rsem.at[s if r is None else r],
            device_id=dev, device_id_type=MESH,
        )

    lo, hi = slice(256, 512), slice(512, 768)
    c_h = [
        remote(fb.at[2:4, :, lo], fb.at[2:4, :, 768:1024], H0, (w, n - 1)),
        remote(fb.at[2:4, :, hi], fb.at[2:4, :, 0:256], H0 + 1, (w, n + 1)),
    ]
    h_send = [nok[0], nok[2]]
    h_recv = [nok[2], nok[0]]
    own = slice(256, 768)
    c_d = [
        remote(fb.at[2:4, :, own], fb.at[4:6, :, own], D0, (w - 1, n)),
        remote(fb.at[2:4, :, own], fb.at[0:2, :, own], D0 + 1, (w + 1, n)),
    ]
    d_send = [wok[0], wok[2]]
    d_recv = [wok[2], wok[0]]
    edge = [slice(0, 256), slice(768, 1024)]
    c_g, g_send, g_recv = [], [], []
    for k, (dst, dev) in enumerate((((4, 6), w - 1), ((0, 2), w + 1))):
        for j in range(2):
            c_g.append(
                remote(fb.at[2:4, :, edge[j]], fb.at[dst[0]:dst[1], :, edge[j]], G0 + 2 * k + j, (dev, n))
            )
            g_send.append(jnp.logical_and(d_send[k], nok[2 * j]))
            g_recv.append(jnp.logical_and(d_recv[k], nok[2 * j]))

    def when(cond, f):
        pl.when(cond)(f)

    for k in range(2):
        when(h_send[k], c_h[k].start)
    for k in range(2):
        when(d_send[k], c_d[k].start)

    def shard(m):
        return w3g.at[pl.ds(pl.multiple_of(m * 16, 16), 16), :]

    c_wx = [remote(w3_ref, shard(n), WX0 + k - 1, (w, xmate(k))) for k in range(1, 4)]
    c_wz = remote(w3_ref, shard(n), WZ0, (w, zmate))
    c_wf = [remote(shard(zmate), shard(zmate), WF0 + k - 1, (w, xmate(k))) for k in range(1, 4)]
    order = [n, xmate(1), xmate(2), xmate(3)]
    order = order + [(m + half) % nn for m in order]
    c_wc = [
        remote(w3_ref if k == 0 else shard(m), shard(m), WC0 + k, (w, mate))
        for k, m in enumerate(order)
    ]
    c_wz.start()
    for c in c_wx:
        c.start()
    c_wc[0].start()

    for d in (2, 3):
        for h in range(2, 6):
            stack1(d, h)

    for k in range(2):
        when(h_recv[k], c_h[k].wait_recv)
    for k in range(4):
        when(g_send[k], c_g[k].start)
    for d in (2, 3):
        for h in (0, 1, 6, 7):
            stack1(d, h)
    for k in range(2):
        when(d_recv[k], c_d[k].wait_recv)
    for d in (0, 1, 4, 5):
        for h in range(2, 6):
            stack1(d, h)
    for k in range(4):
        when(g_recv[k], c_g[k].wait_recv)
    for d in (0, 1, 4, 5):
        for h in (0, 1, 6, 7):
            stack1(d, h)

    c_wz.wait_recv()
    for c in c_wf:
        c.start()
    for k in range(3):
        c_wx[k].wait_recv()
    for k in range(1, 5):
        c_wc[k].start()

    lane6 = lax.broadcasted_iota(jnp.int32, (1, 768), 1)
    inside = jnp.logical_and(
        jnp.logical_or(lane6 >= 128, n > 0), jnp.logical_or(lane6 < 640, n < nn - 1)
    )

    def first(d, carry):
        y = jnp.dot(
            w1p[...], xs1[pl.ds(pl.multiple_of(d * 192, 192), 576), :], preferred_element_type=F32
        )
        y = y[0:64, 0:768] + y[64:128, 128:896] + y[128:192, 256:1024]
        level = 2 * w + d - 1
        keep = jnp.logical_and(inside, jnp.logical_and(level >= 0, level < 2 * nw))
        y = jnp.where(keep, jnp.maximum(y, 0.0), 0.0)
        for h in range(6):
            for e, v in enumerate(shifted(y[:, h * 128:(h + 1) * 128], 128)):
                xs2[pl.ds(pl.multiple_of(d * 192 + e * 64, 64), 64), h * 128:(h + 1) * 128] = v
        return carry

    lax.fori_loop(0, 4, first, 0)

    def second(d):
        y = jnp.dot(w2p[...], xs2[d * 192:d * 192 + 576, :], preferred_element_type=F32)
        return y[0:128, 0:512] + y[128:256, 128:640] + y[256:384, 256:768]

    s = jnp.maximum(jnp.maximum(second(0), second(1)), 0.0)
    rows = []
    for r in range(2):
        t = jnp.maximum(s[:, r * 256:r * 256 + 128], s[:, r * 256 + 128:r * 256 + 256])
        rows.append(jnp.maximum(t, pltpu.roll(t, 127, 1)).astype(BF))
    k_i = lax.broadcasted_iota(jnp.int32, (128, 128), 0)
    j_i = lax.broadcasted_iota(jnp.int32, (128, 128), 1)
    pick0 = jnp.where(k_i == 2 * j_i, 1.0, 0.0).astype(BF)
    pick1 = jnp.where(k_i == 2 * (j_i - 64), 1.0, 0.0).astype(BF)
    pooled = jnp.dot(rows[0], pick0, preferred_element_type=F32) + jnp.dot(
        rows[1], pick1, preferred_element_type=F32
    )
    pb[1, 1] = pooled.astype(BF)

    c_p = []
    for k, (i, j) in enumerate(near):
        c_p.append(
            remote(pb.at[1, 1], pb.at[2 - i, 2 - j], P0 + k, (w + side(i), n + side(j)))
        )
        when(ok(i, j), c_p[k].start)

    for c in c_wf:
        c.wait_recv()
    for k in range(5, 8):
        c_wc[k].start()

    for k, (i, j) in enumerate(near):
        when(ok(2 - i, 2 - j), c_p[k].wait_recv)

    low = lane < 64

    def coarse_stack(a, carry):
        left = pb[a, 0].astype(F32)
        mid = pb[a, 1].astype(F32)
        right = pb[a, 2].astype(F32)
        tops = (
            pltpu.roll(jnp.where(low, mid, left), 64, 1),
            mid,
            pltpu.roll(jnp.where(low, right, mid), 64, 1),
        )
        for b, t in enumerate(tops):
            for e, v in enumerate(shifted(t, 64)):
                xs3[pl.ds(pl.multiple_of(a * 1152 + (b * 3 + e) * 128, 128), 128), :] = v
        return carry

    lax.fori_loop(0, 3, coarse_stack, 0)

    for c in c_wc:
        c.wait_recv()

    def coarse(g, carry):
        y = jnp.dot(
            w3g[pl.ds(pl.multiple_of(g * 128, 128), 128), :], xs3[...], preferred_element_type=F32
        )
        ob[pl.ds(pl.multiple_of(g * 128, 128), 128), :] = jnp.maximum(y, 0.0).astype(BF)
        return carry

    lax.fori_loop(0, 2, coarse, 0)

    def block(m):
        return out_ref.at[:, pl.ds(pl.multiple_of(m * 128, 128), 128)]

    def piece(m):
        return ob.at[pl.ds(pl.multiple_of(m * 16, 16), 16), :]

    c_a = []
    for k in range(1, nn):
        m = (n + k) % nn
        c = remote(piece(m), block(n), A0 + k, (w, m))
        c.start()
        c_a.append(c)
    out_ref[:, pl.ds(pl.multiple_of(n * 128, 128), 128)] = ob[
        pl.ds(pl.multiple_of(n * 16, 16), 16), :
    ]

    for k in range(1, nn):
        src = (n - k + nn) % nn
        remote(piece(n), block(src), A0 + k, (w, src)).wait_recv()

    for k in range(2):
        when(h_send[k], c_h[k].wait_send)
        when(d_send[k], c_d[k].wait_send)
    for k in range(4):
        when(g_send[k], c_g[k].wait_send)
    for k, (i, j) in enumerate(near):
        when(ok(i, j), c_p[k].wait_send)
    c_wz.wait_send()
    for c in c_wx + c_wf + c_wc + c_a:
        c.wait_send()


def solution(mesh):
    nw, nn = mesh.shape["wide"], mesh.shape["narrow"]

    def body(stored_features, channel_scale, channel_shift, first_weight, second_weight, third_weight):
        x = stored_features.reshape(512, 128)
        out = pl.pallas_call(
            functools.partial(kernel, nw, nn),
            out_shape=jax.ShapeDtypeStruct((16, nn * 128), BF),
            in_specs=[pl.BlockSpec(memory_space=pltpu.VMEM)] * 6,
            out_specs=pl.BlockSpec(memory_space=pltpu.VMEM),
            scratch_shapes=[
                pltpu.VMEM((512, 128), F32),
                pltpu.VMEM((6, 64, 1024), BF),
                pltpu.VMEM((6 * 192, 1024), BF),
                pltpu.VMEM((4 * 192, 768), BF),
                pltpu.VMEM((192, 576), BF),
                pltpu.VMEM((384, 576), BF),
                pltpu.VMEM((3, 3, 128, 128), BF),
                pltpu.VMEM((3456, 128), BF),
                pltpu.VMEM((nn * 16, 3456), BF),
                pltpu.VMEM((256, 128), BF),
                pltpu.SemaphoreType.DMA((NSEM,)),
                pltpu.SemaphoreType.DMA((NSEM,)),
            ],
            compiler_params=pltpu.CompilerParams(collective_id=0, has_side_effects=True),
        )(x, channel_scale.reshape(1, 64), channel_shift.reshape(1, 64), first_weight, second_weight, third_weight)
        return out.reshape(16, 1, nn * 128)

    in_specs = (P(None, "wide", "narrow", None), P(), P(), P(), P(), P("narrow", None))
    return jax.shard_map(
        body, mesh=mesh, in_specs=in_specs, out_specs=P("narrow", "wide", None), check_vma=False
    )
```

time: 158 us -> 49.7 us (0.31)
  the two profiles are of different devices: /device:TPU:450 before, /device:TPU:135 now
where the time goes in v1:
time: 49.7 us; the launch traced here: 49.5 us
  Pallas kernels  46 us (93%)
  local copies, waits for them, and re-layouts  3.46 us (7%)
    pallas_call x1, Pallas kernels, body(): pl.pallas_call(functools.partial(kernel, nw, nn), out_shape=jax.ShapeDtyp...  46 us
    unnamed x2, local copies, waits for them, and re-layouts  3.46 us

profile of v1, /device:TPU:135, one launch (start us, length us, event | category | flops | bytes accessed | tf_op | source)
XLA Modules:
  0.0 49.5 jit_solution(5190466474111326910)
XLA Ops:
  0.0 2.0 %copy.7.w2_ref = bf16[128,1728]{1,0:T(8,128)(2,1)} copy(bf16[128,1728]{0,1:T(8,128)(2,1)} %param.10) | data formatting | bytes 884736 | tf_op args[4]
  2.0 46.0 %shard_map.64 = bf16[16,2048]{1,0:T(8,128)(2,1)} custom-call(bf16[512,128]{1,0:T(8,128)(2,1)} %bitcast.5, f32[1,64]{1,0:T(1,128)} %bitcast.6, f32[1,64]{1,0:T(1,128)} %bitcast.7, bf16[64,1728]{1,0:T(8,128)(2,1)} %w1_ref.1, bf16[128,1728]{1,0:T(8,128)(2,1)} %copy.7.w2_ref, bf16[16,3456]{1,0:T(8,128)(2,1)} %w3_ref.1), custom_call_target="tpu_custom_call" | custom-call | tf_op jit(solution)/shard_map/pallas_call | solution.py:323
  48.0 1.5 %copy.9 = bf16[16,1,2048]{2,0,1:T(8,128)(2,1)} copy(bf16[16,1,2048]{2,0,1:T(8,128)(2,1)} %bitcast.4) | data formatting | bytes 131072

commit v2 on v1

--- a/solution.py
+++ b/solution.py
@@ -16,7 +16,7 @@
 
 
 def kernel(nw, nn, x_ref, sc_ref, sh_ref, w1_ref, w2_ref, w3_ref, out_ref,
-           xf, fb, xs1, xs2, w1p, w2p, pb, xs3, w3g, ob, ssem, rsem):
+           xf, fb, xs1, xs2, w1p, w2p, pb, xs3, w3g, ob, ssem, rsem, fsem):
     w = lax.axis_index("wide")
     n = lax.axis_index("narrow")
     half = nn // 2
@@ -43,22 +43,44 @@
 
     near = [(i, j) for i in range(3) for j in range(3) if (i, j) != (1, 1)]
 
+    early = zh == 0
+    late = zh == 1
+    flip = (nw // 8 - 1 - w // 8) * 8 + w % 8 if nw % 8 == 0 else w
+    cross = [jnp.logical_and(n == half, late), None, jnp.logical_and(n == half - 1, early)]
+    same = [jnp.logical_and(nok[0], jnp.logical_not(cross[0])), None, jnp.logical_and(nok[2], jnp.logical_not(cross[2]))]
+
+    def greet(sem, *dev):
+        pl.semaphore_signal(sem, inc=1, device_id=dev, device_id_type=MESH)
+
     barrier = pltpu.get_barrier_semaphore()
-    for k in range(1, nn):
-        pl.semaphore_signal(barrier, inc=1, device_id=(w, (n + k) % nn), device_id_type=MESH)
+    for k in range(1, half):
+        greet(barrier, w, zh * half + (within + k) % half)
     for i in (0, 2):
-        for j in range(3):
-            @pl.when(ok(i, j))
+        @pl.when(wok[i])
+        def _():
+            greet(barrier, w + side(i), n)
+        for j in (0, 2):
+            @pl.when(jnp.logical_and(wok[i], same[j]))
             def _():
-                pl.semaphore_signal(
-                    barrier, inc=1, device_id=(w + side(i), n + side(j)), device_id_type=MESH
-                )
-
-    one = jnp.int32(1)
-    zero = jnp.int32(0)
-    wcount = jnp.where(w > 0, one, zero) + jnp.where(w < nw - 1, one, zero)
-    ncount = jnp.where(n > 0, one, zero) + jnp.where(n < nn - 1, one, zero)
-    expected = (nn - 1) + wcount * (1 + ncount)
+                greet(barrier, w + side(i), n + side(j))
+
+    @pl.when(early)
+    def _():
+        greet(barrier, flip, zmate)
+        for k in range(half):
+            greet(barrier, w, half + (within + k) % half)
+
+    for i in (0, 2):
+        @pl.when(jnp.logical_and(wok[i], cross[2]))
+        def _():
+            greet(barrier, w + side(i), n + 1)
+
+    def count(cond):
+        return jnp.where(cond, jnp.int32(1), jnp.int32(0))
+
+    wcount = count(wok[0]) + count(wok[2])
+    expected = half - 1 + wcount * (1 + count(same[0]) + count(same[2]))
+    expected = expected + count(late) * (half + 1) + count(cross[0]) * wcount
 
     @pl.when(n == 0)
     def _():
@@ -106,14 +128,27 @@
             t = xf[pl.ds(d * 4 + h, 64, stride=8), :]
             fb[2 + d, :, (2 + h) * 128:(3 + h) * 128] = (t * scale + shift).astype(BF)
 
-    for a in range(3):
-        for b in range(3):
-            c0 = (a * 3 + b) * 192
-            w1p[b * 64:(b + 1) * 64, a * 192:(a + 1) * 192] = w1_ref[:, c0:c0 + 192]
-            w2p[b * 128:(b + 1) * 128, a * 192:(a + 1) * 192] = w2_ref[:, c0:c0 + 192]
     w3g[pl.ds(pl.multiple_of(n * 16, 16), 16), :] = w3_ref[...]
 
     pl.semaphore_wait(barrier, expected)
+
+    @pl.when(late)
+    def _():
+        greet(fsem.at[1], flip, zmate)
+
+    @pl.when(cross[0])
+    def _():
+        greet(fsem.at[0], w, n - 1)
+
+    for k in range(half):
+        @pl.when(jnp.logical_and(late, jnp.logical_or(n != half, k != half - 1)))
+        def _():
+            greet(fsem.at[2], w, (within + k) % half)
+
+    for i in (0, 2):
+        @pl.when(jnp.logical_and(wok[i], cross[0]))
+        def _():
+            greet(fsem.at[2], w + side(i), n - 1)
 
     def remote(src, dst, s, dev, r=None):
         return pltpu.make_async_remote_copy(
@@ -148,8 +183,9 @@
     def when(cond, f):
         pl.when(cond)(f)
 
-    for k in range(2):
-        when(h_send[k], c_h[k].start)
+    when(same[0], c_h[0].start)
+    when(same[2], c_h[1].start)
+    when(cross[0], c_h[0].start)
     for k in range(2):
         when(d_send[k], c_d[k].start)
 
@@ -157,7 +193,7 @@
         return w3g.at[pl.ds(pl.multiple_of(m * 16, 16), 16), :]
 
     c_wx = [remote(w3_ref, shard(n), WX0 + k - 1, (w, xmate(k))) for k in range(1, 4)]
-    c_wz = remote(w3_ref, shard(n), WZ0, (w, zmate))
+    c_wz = remote(w3_ref, shard(n), WZ0, (flip, zmate))
     c_wf = [remote(shard(zmate), shard(zmate), WF0 + k - 1, (w, xmate(k))) for k in range(1, 4)]
     order = [n, xmate(1), xmate(2), xmate(3)]
     order = order + [(m + half) % nn for m in order]
@@ -165,40 +201,77 @@
         remote(w3_ref if k == 0 else shard(m), shard(m), WC0 + k, (w, mate))
         for k, m in enumerate(order)
     ]
-    c_wz.start()
+    when(late, c_wz.start)
     for c in c_wx:
         c.start()
     c_wc[0].start()
 
+    for a in range(3):
+        for b in range(3):
+            c0 = (a * 3 + b) * 192
+            w1p[b * 64:(b + 1) * 64, a * 192:(a + 1) * 192] = w1_ref[:, c0:c0 + 192]
+            w2p[b * 128:(b + 1) * 128, a * 192:(a + 1) * 192] = w2_ref[c0:c0 + 192, :].T
     for d in (2, 3):
         for h in range(2, 6):
             stack1(d, h)
 
-    for k in range(2):
-        when(h_recv[k], c_h[k].wait_recv)
-    for k in range(4):
-        when(g_send[k], c_g[k].start)
-    for d in (2, 3):
-        for h in (0, 1, 6, 7):
-            stack1(d, h)
+    def edge_rows(depths, j):
+        for d in depths:
+            for h in ((0, 1), (6, 7))[j]:
+                stack1(d, h)
+
+    def forward(j, cond):
+        for k in range(2):
+            when(jnp.logical_and(cond, d_send[k]), c_g[2 * k + j].start)
+
+    for j in range(2):
+        when(same[2 * j], c_h[1 - j].wait_recv)
+        forward(j, same[2 * j])
+    @pl.when(cross[2])
+    def _():
+        pl.semaphore_wait(fsem.at[0], 1)
+        c_h[1].start()
+
+    @pl.when(early)
+    def _():
+        pl.semaphore_wait(fsem.at[1], 1)
+        c_wz.start()
+
+    for j in range(2):
+        @pl.when(jnp.logical_not(cross[2 * j]))
+        def _():
+            edge_rows((2, 3), j)
     for k in range(2):
         when(d_recv[k], c_d[k].wait_recv)
     for d in (0, 1, 4, 5):
         for h in range(2, 6):
             stack1(d, h)
-    for k in range(4):
-        when(g_recv[k], c_g[k].wait_recv)
-    for d in (0, 1, 4, 5):
-        for h in (0, 1, 6, 7):
-            stack1(d, h)
-
-    c_wz.wait_recv()
-    for c in c_wf:
-        c.start()
-    for k in range(3):
-        c_wx[k].wait_recv()
-    for k in range(1, 5):
-        c_wc[k].start()
+    for j in range(2):
+        for k in range(2):
+            when(jnp.logical_and(same[2 * j], d_recv[k]), c_g[2 * k + j].wait_recv)
+        @pl.when(jnp.logical_not(cross[2 * j]))
+        def _():
+            edge_rows((0, 1, 4, 5), j)
+    for j in range(2):
+        @pl.when(cross[2 * j])
+        def _():
+            c_h[1 - j].wait_recv()
+            forward(j, cross[2 * j])
+            edge_rows((2, 3), j)
+            for k in range(2):
+                when(d_recv[k], c_g[2 * k + j].wait_recv)
+            edge_rows((0, 1, 4, 5), j)
+
+    def spread():
+        c_wz.wait_recv()
+        for c in c_wf:
+            c.start()
+        for k in range(3):
+            c_wx[k].wait_recv()
+        for k in range(1, 5):
+            c_wc[k].start()
+
+    when(cross[0], spread)
 
     lane6 = lax.broadcasted_iota(jnp.int32, (1, 768), 1)
     inside = jnp.logical_and(
@@ -238,6 +311,10 @@
     )
     pb[1, 1] = pooled.astype(BF)
 
+    @pl.when(early)
+    def _():
+        pl.semaphore_wait(fsem.at[2], half - count(cross[2]) + count(cross[2]) * wcount)
+
     c_p = []
     for k, (i, j) in enumerate(near):
         c_p.append(
@@ -245,6 +322,7 @@
         )
         when(ok(i, j), c_p[k].start)
 
+    when(jnp.logical_not(cross[0]), spread)
     for c in c_wf:
         c.wait_recv()
     for k in range(5, 8):
@@ -322,7 +400,7 @@
         x = stored_features.reshape(512, 128)
         out = pl.pallas_call(
             functools.partial(kernel, nw, nn),
-            out_shape=jax.ShapeDtypeStruct((16, nn * 128), BF),
+            out_shape=pltpu.VMEM((16, nn * 128), BF),
             in_specs=[pl.BlockSpec(memory_space=pltpu.VMEM)] * 6,
             out_specs=pl.BlockSpec(memory_space=pltpu.VMEM),
             scratch_shapes=[
@@ -338,9 +416,10 @@
                 pltpu.VMEM((256, 128), BF),
                 pltpu.SemaphoreType.DMA((NSEM,)),
                 pltpu.SemaphoreType.DMA((NSEM,)),
+                pltpu.SemaphoreType.REGULAR((3,)),
             ],
             compiler_params=pltpu.CompilerParams(collective_id=0, has_side_effects=True),
-        )(x, channel_scale.reshape(1, 64), channel_shift.reshape(1, 64), first_weight, second_weight, third_weight)
+        )(x, channel_scale.reshape(1, 64), channel_shift.reshape(1, 64), first_weight, second_weight.T, third_weight)
         return out.reshape(16, 1, nn * 128)
 
     in_specs = (P(None, "wide", "narrow", None), P(), P(), P(), P(), P("narrow", None))

time: 49.7 us -> 44.3 us (0.89)
  the two profiles are of different devices: /device:TPU:135 before, /device:TPU:127 now
where the time goes in v2:
time: 44.3 us; the launch traced here: 44.1 us
  Pallas kernels  43.5 us (98%)
  local copies, waits for them, and re-layouts  0.63 us (1%)
    pallas_call x1, Pallas kernels, body(): pl.pallas_call(functools.partial(kernel, nw, nn), out_shape=pltpu.VMEM((1...  43.5 us

profile of v2, /device:TPU:127, one launch (start us, length us, event | category | flops | bytes accessed | tf_op | source)
XLA Modules:
  0.0 44.1 jit_solution(16893858525251208406)
XLA Ops:
  0.0 43.5 %shard_map.64 = bf16[16,2048]{1,0:T(8,128)(2,1)S(1)} custom-call(bf16[512,128]{1,0:T(8,128)(2,1)} %bitcast.7, f32[1,64]{1,0:T(1,128)} %bitcast.8, f32[1,64]{1,0:T(1,128)} %bitcast.9, bf16[64,1728]{1,0:T(8,128)(2,1)} %w1_ref.1, bf16[1728,128]{1,0:T(8,128)(2,1)} %bitcast.6, bf16[16,3456]{1,0:T(8,128)(2,1)} %w3_ref.1), custom_call_target="tpu_custom_call" | custom-call | tf_op jit(solution)/shard_map/pallas_call | solution.py:401
  43.5 0.6 %copy.8 = bf16[16,1,2048]{2,0,1:T(8,128)(2,1)} copy(bf16[16,1,2048]{2,0,1:T(8,128)(2,1)S(1)} %bitcast.5) | data formatting | bytes 131072

commit v3 on v2

v3 whole, which is shorter than its diff:
```python
import functools

import jax
import jax.numpy as jnp
from jax import lax
from jax.experimental import pallas as pl
from jax.experimental.pallas import tpu as pltpu
from jax.sharding import PartitionSpec as P

BF = jnp.bfloat16
F32 = jnp.float32
MESH = pl.DeviceIdType.MESH
SPREAD = 0

names = dict(H=2, D=2, G=4, P=8, WX=3, WZ=2, WF=6, WC=8, A=16, X=3, E=2, B=16, L=6)
BASE, NSEM = {}, 0
for name, size in names.items():
    BASE[name] = NSEM
    NSEM += size
H0, D0, G0, P0, WX0, WZ0, WF0, WC0, A0, X0, E0, B0, L0 = BASE.values()


def kernel(nw, nn, x_hbm, sc_hbm, sh_hbm, w1_hbm, w2_hbm, w3_hbm, out_ref,
           x_ref, sc_ref, sh_ref, w1_ref, w2_ref, xf, fb, xs1, xs2, w1p, w2p, pb, xs3, w3g, ob, rb, xs4, of, px, ssem, rsem, fsem):
    w = lax.axis_index("wide")
    n = lax.axis_index("narrow")
    half = nn // 2
    zh = n // half
    within = n % half
    mate = n + 1 - 2 * (n % 2)
    zmate = (n + half) % nn

    def xmate(k):
        return zh * half + (within + 2 * k) % half

    def side(i):
        return i - 1

    wok = [w > 0, None, w < nw - 1]
    nok = [n > 0, None, n < nn - 1]

    def ok(i, j):
        if i == 1:
            return nok[j]
        if j == 1:
            return wok[i]
        return jnp.logical_and(wok[i], nok[j])

    near = [(i, j) for i in range(3) for j in range(3) if (i, j) != (1, 1)]

    early = zh == 0
    late = zh == 1
    flip = (nw // 8 - 1 - w // 8) * 8 + w % 8 if nw % 8 == 0 else w
    cross = [jnp.logical_and(n == half, late), None, jnp.logical_and(n == half - 1, early)]
    same = [jnp.logical_and(nok[0], jnp.logical_not(cross[0])), None, jnp.logical_and(nok[2], jnp.logical_not(cross[2]))]

    def greet(sem, *dev):
        pl.semaphore_signal(sem, inc=1, device_id=dev, device_id_type=MESH)

    barrier = pltpu.get_barrier_semaphore()
    for k in range(1, half):
        greet(barrier, w, zh * half + (within + k) % half)
    for i in (0, 2):
        @pl.when(wok[i])
        def _():
            greet(barrier, w + side(i), n)
        for j in (0, 2):
            @pl.when(jnp.logical_and(wok[i], same[j]))
            def _():
                greet(barrier, w + side(i), n + side(j))

    @pl.when(early)
    def _():
        greet(barrier, flip, zmate)
        for k in range(half):
            greet(barrier, w, half + (within + k) % half)

    def count(cond):
        return jnp.where(cond, jnp.int32(1), jnp.int32(0))

    wcount = count(wok[0]) + count(wok[2])
    expected = half - 1 + wcount * (1 + count(same[0]) + count(same[2]))
    expected = expected + count(late) * (half + 1)

    mine = pl.ds(pl.multiple_of(n * 16, 16), 16)
    loads = [
        pltpu.make_async_copy(src, dst, rsem.at[L0 + k])
        for k, (src, dst) in enumerate((
            (x_hbm, x_ref), (sc_hbm, sc_ref), (sh_hbm, sh_ref),
            (w3_hbm, w3g.at[mine, :]), (w1_hbm, w1_ref), (w2_hbm, w2_ref),
        ))
    ]
    for c in loads:
        c.start()

    @pl.when(jnp.logical_or(n == 0, n == half))
    def _():
        fb[:, :, 0:256] = jnp.zeros((6, 64, 256), BF)
        pb[:, 0] = jnp.zeros((3, 128, 128), BF)

    @pl.when(n == nn - 1)
    def _():
        fb[:, :, 768:1024] = jnp.zeros((6, 64, 256), BF)
        pb[:, 2] = jnp.zeros((3, 128, 128), BF)

    @pl.when(w == 0)
    def _():
        fb[0:2] = jnp.zeros((2, 64, 1280), BF)
        pb[0] = jnp.zeros((3, 128, 128), BF)

    @pl.when(w == nw - 1)
    def _():
        fb[4:6] = jnp.zeros((2, 64, 1280), BF)
        pb[2] = jnp.zeros((3, 128, 128), BF)

    lane = lax.broadcasted_iota(jnp.int32, (1, 128), 1)

    def shifted(t, period):
        pos = lane % period
        before = jnp.where(pos > 0, pltpu.roll(t, 1, 1), 0.0)
        after = jnp.where(pos < period - 1, pltpu.roll(t, 127, 1), 0.0)
        return before.astype(BF), t.astype(BF), after.astype(BF)

    def stack1(d, h):
        t = fb[d, :, h * 128:(h + 1) * 128].astype(F32)
        for e, v in enumerate(shifted(t, 128)):
            xs1[d * 192 + e * 64:d * 192 + (e + 1) * 64, h * 128:(h + 1) * 128] = v

    eye = lax.broadcasted_iota(jnp.int32, (64, 64), 0) == lax.broadcasted_iota(jnp.int32, (64, 64), 1)

    def column(ref):
        return jnp.sum(jnp.where(eye, ref[...], 0.0), axis=1, keepdims=True)

    for c in loads[:3]:
        c.wait()
    scale = column(sc_ref)
    shift = column(sh_ref)
    xf[...] = x_ref[...].astype(F32)
    for d in range(2):
        for h in range(4):
            t = xf[pl.ds(d * 4 + h, 64, stride=8), :]
            fb[2 + d, :, (2 + h) * 128:(3 + h) * 128] = (t * scale + shift).astype(BF)

    loads[3].wait()
    pl.semaphore_wait(barrier, expected)

    @pl.when(late)
    def _():
        greet(fsem.at[0], flip, zmate)
        for k in range(half):
            greet(fsem.at[1], w, (within + k) % half)

    def remote(src, dst, s, dev, r=None):
        return pltpu.make_async_remote_copy(
            src_ref=src, dst_ref=dst, send_sem=ssem.at[s], recv_sem=rsem.at[s if r is None else r],
            device_id=dev, device_id_type=MESH,
        )

    lo, hi = slice(256, 512), slice(512, 768)
    c_h = [
        remote(fb.at[2:4, :, lo], fb.at[2:4, :, 768:1024], H0, (w, n - 1)),
        remote(fb.at[2:4, :, hi], fb.at[2:4, :, 0:256], H0 + 1, (w, n + 1)),
    ]
    own = slice(256, 768)
    c_d = [
        remote(fb.at[2:4, :, own], fb.at[4:6, :, own], D0, (w - 1, n)),
        remote(fb.at[2:4, :, own], fb.at[0:2, :, own], D0 + 1, (w + 1, n)),
    ]
    d_send = [wok[0], wok[2]]
    d_recv = [wok[2], wok[0]]
    edge = [slice(0, 256), slice(768, 1024)]
    c_g, g_send, g_recv = [], [], []
    for k, (dst, dev) in enumerate((((4, 6), w - 1), ((0, 2), w + 1))):
        for j in range(2):
            c_g.append(
                remote(fb.at[2:4, :, edge[j]], fb.at[dst[0]:dst[1], :, edge[j]], G0 + 2 * k + j, (dev, n))
            )
            g_send.append(jnp.logical_and(d_send[k], same[2 * j]))
            g_recv.append(jnp.logical_and(d_recv[k], same[2 * j]))

    far = slice(768, 1280)
    c_x = [
        remote(fb.at[2:4, :, own], fb.at[2:4, :, far], X0, (w, n - 1)),
        remote(fb.at[2:4, :, far], fb.at[4:6, :, far], X0 + 1, (w - 1, n)),
        remote(fb.at[2:4, :, far], fb.at[0:2, :, far], X0 + 2, (w + 1, n)),
    ]

    def when(cond, f):
        pl.when(cond)(f)

    upper = cross[2]
    lower = cross[0]
    when(lower, c_x[0].start)
    when(same[0], c_h[0].start)
    when(same[2], c_h[1].start)
    for k in range(2):
        when(d_send[k], c_d[k].start)

    def shard(m):
        return w3g.at[pl.ds(pl.multiple_of(m * 16, 16), 16), :]

    c_wx = [remote(shard(n), shard(n), WX0 + k - 1, (w, xmate(k))) for k in range(1, 4)]

    def half_shard(m, q):
        return w3g.at[pl.ds(pl.multiple_of(m * 16, 16), 16), (slice(0, 1792), slice(1792, 3456))[q]]

    c_wz = [remote(half_shard(n, q), half_shard(n, q), WZ0 + q, (flip, zmate)) for q in range(2)]
    c_wf = [
        [
            remote(half_shard(zmate, q), half_shard(zmate, q), WF0 + 3 * q + k - 1, (w, xmate(k)))
            for k in range(1, 4)
        ]
        for q in range(2)
    ]
    order = [n, xmate(1), xmate(2), xmate(3)]
    order = order + [(m + half) % nn for m in order]
    c_wc = [remote(shard(m), shard(m), WC0 + k, (w, mate)) for k, m in enumerate(order)]
    for q in range(2):
        when(late, c_wz[q].start)
    for c in c_wx:
        c.start()
    c_wc[0].start()

    loads[4].wait()
    loads[5].wait()
    for a in range(3):
        for b in range(3):
            c0 = (a * 3 + b) * 192
            w1p[b * 64:(b + 1) * 64, a * 192:(a + 1) * 192] = w1_ref[:, c0:c0 + 192]
            w2p[b * 128:(b + 1) * 128, a * 192:(a + 1) * 192] = w2_ref[c0:c0 + 192, :].T
    for d in (2, 3):
        for h in range(2, 6):
            stack1(d, h)

    def edge_rows(depths, j):
        for d in depths:
            for h in ((0, 1), (6, 7))[j]:
                stack1(d, h)

    def forward(j, cond):
        for k in range(2):
            when(jnp.logical_and(cond, d_send[k]), c_g[2 * k + j].start)

    for j in range(2):
        when(same[2 * j], c_h[1 - j].wait_recv)
        forward(j, same[2 * j])
    @pl.when(early)
    def _():
        pl.semaphore_wait(fsem.at[0], 1)
        for c in c_wz:
            c.start()

    edge_rows((2, 3), 0)
    when(jnp.logical_not(upper), lambda: edge_rows((2, 3), 1))
    for k in range(2):
        when(d_recv[k], c_d[k].wait_recv)
    for d in (0, 1, 4, 5):
        for h in range(2, 6):
            stack1(d, h)
    for k in range(4):
        when(g_recv[k], c_g[k].wait_recv)
    edge_rows((0, 1, 4, 5), 0)
    when(jnp.logical_not(upper), lambda: edge_rows((0, 1, 4, 5), 1))

    def spread():
        for q in range(2):
            c_wz[q].wait_recv()
            for c in c_wf[q]:
                c.start()
        for k in range(3):
            c_wx[k].wait_recv()
        for k in range(1, 5):
            c_wc[k].start()

    def first(h0, rows):
        row = h0 * 128 + lax.broadcasted_iota(jnp.int32, (1, rows * 128), 1)
        inside = jnp.logical_and(
            jnp.logical_or(row >= 128, n > 0), jnp.logical_or(row < 640, n < nn - 1)
        )
        span = rows * 128

        def level(d, carry):
            y = jnp.dot(
                w1p[...],
                xs1[pl.ds(pl.multiple_of(d * 192, 192), 576), h0 * 128:h0 * 128 + span + 256],
                preferred_element_type=F32,
            )
            y = y[0:64, 0:span] + y[64:128, 128:span + 128] + y[128:192, 256:span + 256]
            depth = 2 * w + d - 1
            keep = jnp.logical_and(inside, jnp.logical_and(depth >= 0, depth < 2 * nw))
            y = jnp.where(keep, jnp.maximum(y, 0.0), 0.0)
            for h in range(rows):
                for e, v in enumerate(shifted(y[:, h * 128:(h + 1) * 128], 128)):
                    c0 = (h0 + h) * 128
                    xs2[pl.ds(pl.multiple_of(d * 192 + e * 64, 64), 64), c0:c0 + 128] = v
            return carry

        lax.fori_loop(0, 4, level, 0)

    def second(h0, rows):
        span = rows * 128

        def level(d):
            y = jnp.dot(
                w2p[...], xs2[d * 192:d * 192 + 576, h0 * 128:h0 * 128 + span + 256],
                preferred_element_type=F32,
            )
            return y[0:128, 0:span] + y[128:256, 128:span + 128] + y[256:384, 256:span + 256]

        s = jnp.maximum(jnp.maximum(level(0), level(1)), 0.0)
        out = []
        for r in range(rows // 2):
            t = jnp.maximum(s[:, r * 256:r * 256 + 128], s[:, r * 256 + 128:r * 256 + 256])
            out.append(jnp.maximum(t, pltpu.roll(t, 127, 1)).astype(BF))
        return out

    k_i = lax.broadcasted_iota(jnp.int32, (128, 128), 0)
    j_i = lax.broadcasted_iota(jnp.int32, (128, 128), 1)

    def pick(t, place):
        cells = jnp.where(k_i == 2 * (j_i - 64 * place), 1.0, 0.0).astype(BF)
        return jnp.dot(t, cells, preferred_element_type=F32)

    @pl.when(jnp.logical_not(upper))
    def _():
        if SPREAD == 0:
            spread()
        first(0, 6)
        if SPREAD == 1:
            spread()
        r0, r1 = second(0, 4)
        keep = jnp.where(lower, 0.0, 1.0)
        pb[1, 1] = (pick(r0, 0) * keep + pick(r1, 1)).astype(BF)

    @pl.when(upper)
    def _():
        c_x[0].wait_recv()
        for k in range(2):
            when(d_send[k], c_x[1 + k].start)
        if SPREAD == 0:
            spread()
        for d in (2, 3):
            for h in range(6, 10):
                stack1(d, h)
        first(0, 4)
        if SPREAD == 1:
            spread()
        rb[...] = second(0, 2)[0]
        for k in range(2):
            when(d_recv[k], c_x[1 + k].wait_recv)
        for d in (0, 1, 4, 5):
            for h in range(6, 10):
                stack1(d, h)
        first(4, 4)
        r1, r2 = second(2, 4)
        pb[1, 1] = (pick(rb[...], 0) + pick(r1, 1)).astype(BF)
        pb[1, 2] = pick(r2, 0).astype(BF)

    def beside(i, j):
        if j == 1:
            return wok[i]
        if i == 1:
            return same[j]
        return jnp.logical_and(wok[i], same[j])

    c_e = [
        remote(pb.at[1, 2], pb.at[2, 2], E0, (w - 1, n)),
        remote(pb.at[1, 2], pb.at[0, 2], E0 + 1, (w + 1, n)),
    ]
    for k in range(2):
        when(jnp.logical_and(upper, d_send[k]), c_e[k].start)
    c_p = []
    for k, (i, j) in enumerate(near):
        c_p.append(
            remote(pb.at[1, 1], pb.at[2 - i, 2 - j], P0 + k, (w + side(i), n + side(j)))
        )
        when(beside(i, j), c_p[k].start)

    if SPREAD == 2:
        spread()
    for c in c_wf[0] + c_wf[1]:
        c.wait_recv()
    for k in range(5, 8):
        c_wc[k].start()

    for k, (i, j) in enumerate(near):
        when(beside(2 - i, 2 - j), c_p[k].wait_recv)

    low = lane < 64

    @pl.when(upper)
    def _():
        for k in range(2):
            when(d_recv[k], c_e[k].wait_recv)

    def coarse_stack(left_of, mid_of, right_of, dst):
        def level(a, carry):
            left = left_of(a).astype(F32)
            mid = mid_of(a).astype(F32)
            right = right_of(a).astype(F32)
            tops = (
                pltpu.roll(jnp.where(low, mid, left), 64, 1),
                mid,
                pltpu.roll(jnp.where(low, right, mid), 64, 1),
            )
            for b, t in enumerate(tops):
                for e, v in enumerate(shifted(t, 64)):
                    dst[pl.ds(pl.multiple_of(a * 1152 + (b * 3 + e) * 128, 128), 128), :] = v
            return carry

        lax.fori_loop(0, 3, level, 0)

    coarse_stack(lambda a: pb[a, 0], lambda a: pb[a, 1], lambda a: pb[a, 2], xs3)
    blank = jnp.zeros((128, 128), F32)
    when(upper, lambda: coarse_stack(lambda a: pb[a, 1], lambda a: pb[a, 2], lambda a: blank, xs4))

    for c in c_wc:
        c.wait_recv()

    def coarse(src, whole):
        def part(g, carry):
            rows = pl.ds(pl.multiple_of(g * 128, 128), 128)
            y = jnp.dot(w3g[rows, :], src[...], preferred_element_type=F32)
            if whole:
                ob[rows, :] = jnp.maximum(y, 0.0).astype(BF)
            else:
                of[rows, :] = y
            return carry

        lax.fori_loop(0, 2, part, 0)

    when(jnp.logical_not(lower), lambda: coarse(xs3, True))
    when(lower, lambda: coarse(xs3, False))
    when(upper, lambda: coarse(xs4, False))

    @pl.when(early)
    def _():
        pl.semaphore_wait(fsem.at[1], half)

    def block(m):
        return out_ref.at[:, pl.ds(pl.multiple_of(m * 128, 128), 128)]

    def piece(ref, m):
        return ref.at[pl.ds(pl.multiple_of(m * 16, 16), 16), :]

    c_a, c_b = [], []
    for k in range(1, nn):
        m = (n + k) % nn
        c_a.append(remote(piece(ob, m), block(n), A0 + k, (w, m)))
        c_b.append([
            remote(piece(of, m), px.at[q], B0 + k, (w, m), r=B0 + q) for q in range(2)
        ])
        when(jnp.logical_not(lower), c_a[-1].start)
        when(upper, c_b[-1][0].start)
        when(lower, c_b[-1][1].start)

    @pl.when(jnp.logical_not(lower))
    def _():
        out_ref[:, pl.ds(pl.multiple_of(n * 128, 128), 128)] = ob[mine, :]

    @pl.when(upper)
    def _():
        px[0] = of[mine, :]

    @pl.when(lower)
    def _():
        px[1] = of[mine, :]

    for k in range(1, nn):
        src = (n - k + nn) % nn
        when(src != half, remote(piece(ob, n), block(src), A0 + k, (w, src)).wait_recv)
    for q, home in enumerate((upper, lower)):
        when(jnp.logical_not(home), remote(piece(of, n), px.at[q], B0 + q, (w, half - 1 + q)).wait_recv)
    out_ref[:, half * 128:(half + 1) * 128] = jnp.maximum(px[0] + px[1], 0.0).astype(BF)

    when(same[0], c_h[0].wait_send)
    when(same[2], c_h[1].wait_send)
    for k in range(2):
        when(d_send[k], c_d[k].wait_send)
    for k in range(4):
        when(g_send[k], c_g[k].wait_send)
    for k, (i, j) in enumerate(near):
        when(beside(i, j), c_p[k].wait_send)
    for c in c_wz + c_wx + c_wf[0] + c_wf[1] + c_wc:
        c.wait_send()

    @pl.when(lower)
    def _():
        c_x[0].wait_send()
        for c in c_b:
            c[1].wait_send()

    @pl.when(upper)
    def _():
        for k in range(2):
            when(d_send[k], c_x[1 + k].wait_send)
            when(d_send[k], c_e[k].wait_send)
        for c in c_b:
            c[0].wait_send()

    @pl.when(jnp.logical_not(lower))
    def _():
        for c in c_a:
            c.wait_send()


def solution(mesh):
    nw, nn = mesh.shape["wide"], mesh.shape["narrow"]

    def body(stored_features, channel_scale, channel_shift, first_weight, second_weight, third_weight):
        x = stored_features.reshape(512, 128)
        out = pl.pallas_call(
            functools.partial(kernel, nw, nn),
            out_shape=pltpu.VMEM((16, nn * 128), BF),
            in_specs=[pl.BlockSpec(memory_space=pl.ANY)] * 6,
            out_specs=pl.BlockSpec(memory_space=pltpu.VMEM),
            scratch_shapes=[
                pltpu.VMEM((512, 128), BF),
                pltpu.VMEM((1, 64), F32),
                pltpu.VMEM((1, 64), F32),
                pltpu.VMEM((64, 1728), BF),
                pltpu.VMEM((1728, 128), BF),
                pltpu.VMEM((512, 128), F32),
                pltpu.VMEM((6, 64, 1280), BF),
                pltpu.VMEM((6 * 192, 1280), BF),
                pltpu.VMEM((4 * 192, 1024), BF),
                pltpu.VMEM((192, 576), BF),
                pltpu.VMEM((384, 576), BF),
                pltpu.VMEM((3, 3, 128, 128), BF),
                pltpu.VMEM((3456, 128), BF),
                pltpu.VMEM((nn * 16, 3456), BF),
                pltpu.VMEM((256, 128), BF),
                pltpu.VMEM((128, 128), BF),
                pltpu.VMEM((3456, 128), BF),
                pltpu.VMEM((256, 128), F32),
                pltpu.VMEM((2, 16, 128), F32),
                pltpu.SemaphoreType.DMA((NSEM,)),
                pltpu.SemaphoreType.DMA((NSEM,)),
                pltpu.SemaphoreType.REGULAR((2,)),
            ],
            compiler_params=pltpu.CompilerParams(collective_id=0, has_side_effects=True),
        )(x, channel_scale.reshape(1, 64), channel_shift.reshape(1, 64), first_weight, second_weight.T, third_weight)
        return out.reshape(16, 1, nn * 128)

    in_specs = (P(None, "wide", "narrow", None), P(), P(), P(), P(), P("narrow", None))
    return jax.shard_map(
        body, mesh=mesh, in_specs=in_specs, out_specs=P("narrow", "wide", None), check_vma=False
    )
```

time: 44.3 us -> 42.2 us (0.953)
  the two profiles are of different devices: /device:TPU:127 before, /device:TPU:129 now
where the time goes in v3:
time: 42.2 us; the launch traced here: 42 us
  Pallas kernels  41.4 us (98%)
  local copies, waits for them, and re-layouts  0.63 us (1%)
    pallas_call x1, Pallas kernels, body(): pl.pallas_call(functools.partial(kernel, nw, nn), out_shape=pltpu.VMEM((1...  41.4 us

profile of v3, /device:TPU:129, one launch (start us, length us, event | category | flops | bytes accessed | tf_op | source)
XLA Modules:
  0.0 42.0 jit_solution(10126127672941203533)
XLA Ops:
  0.0 41.4 %shard_map.64 = bf16[16,2048]{1,0:T(8,128)(2,1)S(1)} custom-call(bf16[512,128]{1,0:T(8,128)(2,1)} %bitcast.7, f32[1,64]{1,0:T(1,128)} %bitcast.8, f32[1,64]{1,0:T(1,128)} %bitcast.9, bf16[64,1728]{1,0:T(8,128)(2,1)} %w1_hbm.1, bf16[1728,128]{1,0:T(8,128)(2,1)} %bitcast.6, bf16[16,3456]{1,0:T(8,128)(2,1)} %w3_hbm.1), custom_call_target="tpu_custom_call" | custom-call | tf_op jit(solution)/shard_map/pallas_call | solution.py:512
  41.4 0.6 %copy.8 = bf16[16,1,2048]{2,0,1:T(8,128)(2,1)} copy(bf16[16,1,2048]{2,0,1:T(8,128)(2,1)S(1)} %bitcast.5) | data formatting | bytes 131072

commit v4 on v3

--- a/solution.py
+++ b/solution.py
@@ -96,22 +96,22 @@
     @pl.when(jnp.logical_or(n == 0, n == half))
     def _():
         fb[:, :, 0:256] = jnp.zeros((6, 64, 256), BF)
-        pb[:, 0] = jnp.zeros((3, 128, 128), BF)
+        pb[:, 0] = jnp.zeros((3, 64, 128), BF)
 
     @pl.when(n == nn - 1)
     def _():
         fb[:, :, 768:1024] = jnp.zeros((6, 64, 256), BF)
-        pb[:, 2] = jnp.zeros((3, 128, 128), BF)
+        pb[:, 3] = jnp.zeros((3, 64, 128), BF)
 
     @pl.when(w == 0)
     def _():
         fb[0:2] = jnp.zeros((2, 64, 1280), BF)
-        pb[0] = jnp.zeros((3, 128, 128), BF)
+        pb[0] = jnp.zeros((4, 64, 128), BF)
 
     @pl.when(w == nw - 1)
     def _():
         fb[4:6] = jnp.zeros((2, 64, 1280), BF)
-        pb[2] = jnp.zeros((3, 128, 128), BF)
+        pb[2] = jnp.zeros((4, 64, 128), BF)
 
     lane = lax.broadcasted_iota(jnp.int32, (1, 128), 1)
 
@@ -168,16 +168,22 @@
     ]
     d_send = [wok[0], wok[2]]
     d_recv = [wok[2], wok[0]]
-    edge = [slice(0, 256), slice(768, 1024)]
-    c_g, g_send, g_recv = [], [], []
-    for k, (dst, dev) in enumerate((((4, 6), w - 1), ((0, 2), w + 1))):
-        for j in range(2):
-            c_g.append(
-                remote(fb.at[2:4, :, edge[j]], fb.at[dst[0]:dst[1], :, edge[j]], G0 + 2 * k + j, (dev, n))
-            )
-            g_send.append(jnp.logical_and(d_send[k], same[2 * j]))
-            g_recv.append(jnp.logical_and(d_recv[k], same[2 * j]))
-
+    even = n % 2 == 0
+    outer = jnp.logical_or(jnp.logical_and(even, same[0]), jnp.logical_and(jnp.logical_not(even), same[2]))
+
+    def rows_at(on_even, on_odd):
+        return pl.ds(pl.multiple_of(jnp.where(even, on_even, on_odd), 256), 256)
+
+    outside = rows_at(0, 768)
+    c_g = [
+        remote(fb.at[2:4, :, outside], fb.at[4:6, :, outside], G0, (w - 1, n)),
+        remote(fb.at[2:4, :, outside], fb.at[0:2, :, outside], G0 + 1, (w + 1, n)),
+    ]
+    depths = (slice(4, 6), slice(0, 2))
+    c_i = [
+        remote(fb.at[depths[k], :, rows_at(512, 256)], fb.at[depths[k], :, rows_at(0, 768)], G0 + 2 + k, (w, mate))
+        for k in range(2)
+    ]
     far = slice(768, 1280)
     c_x = [
         remote(fb.at[2:4, :, own], fb.at[2:4, :, far], X0, (w, n - 1)),
@@ -237,13 +243,10 @@
             for h in ((0, 1), (6, 7))[j]:
                 stack1(d, h)
 
-    def forward(j, cond):
-        for k in range(2):
-            when(jnp.logical_and(cond, d_send[k]), c_g[2 * k + j].start)
-
     for j in range(2):
         when(same[2 * j], c_h[1 - j].wait_recv)
-        forward(j, same[2 * j])
+    for k in range(2):
+        when(jnp.logical_and(outer, d_send[k]), c_g[k].start)
     @pl.when(early)
     def _():
         pl.semaphore_wait(fsem.at[0], 1)
@@ -253,12 +256,16 @@
     edge_rows((2, 3), 0)
     when(jnp.logical_not(upper), lambda: edge_rows((2, 3), 1))
     for k in range(2):
-        when(d_recv[k], c_d[k].wait_recv)
+        @pl.when(d_recv[k])
+        def _():
+            c_d[k].wait_recv()
+            c_i[k].start()
     for d in (0, 1, 4, 5):
         for h in range(2, 6):
             stack1(d, h)
-    for k in range(4):
-        when(g_recv[k], c_g[k].wait_recv)
+    for k in range(2):
+        when(d_recv[k], c_i[k].wait_recv)
+        when(jnp.logical_and(outer, d_recv[k]), c_g[k].wait_recv)
     edge_rows((0, 1, 4, 5), 0)
     when(jnp.logical_not(upper), lambda: edge_rows((0, 1, 4, 5), 1))
 
@@ -317,9 +324,12 @@
     k_i = lax.broadcasted_iota(jnp.int32, (128, 128), 0)
     j_i = lax.broadcasted_iota(jnp.int32, (128, 128), 1)
 
-    def pick(t, place):
-        cells = jnp.where(k_i == 2 * (j_i - 64 * place), 1.0, 0.0).astype(BF)
-        return jnp.dot(t, cells, preferred_element_type=F32)
+    picks = [jnp.where(k_i == 2 * (j_i - 64 * q), 1.0, 0.0).astype(BF) for q in range(2)]
+
+    def pack(t):
+        return jnp.dot(t[0:64], picks[0], preferred_element_type=F32) + jnp.dot(
+            t[64:128], picks[1], preferred_element_type=F32
+        )
 
     @pl.when(jnp.logical_not(upper))
     def _():
@@ -330,7 +340,8 @@
             spread()
         r0, r1 = second(0, 4)
         keep = jnp.where(lower, 0.0, 1.0)
-        pb[1, 1] = (pick(r0, 0) * keep + pick(r1, 1)).astype(BF)
+        pb[1, 1] = (pack(r0) * keep).astype(BF)
+        pb[1, 2] = pack(r1).astype(BF)
 
     @pl.when(upper)
     def _():
@@ -353,8 +364,9 @@
                 stack1(d, h)
         first(4, 4)
         r1, r2 = second(2, 4)
-        pb[1, 1] = (pick(rb[...], 0) + pick(r1, 1)).astype(BF)
-        pb[1, 2] = pick(r2, 0).astype(BF)
+        pb[1, 1] = pack(rb[...]).astype(BF)
+        pb[1, 2] = pack(r1).astype(BF)
+        pb[1, 3] = pack(r2).astype(BF)
 
     def beside(i, j):
         if j == 1:
@@ -364,17 +376,23 @@
         return jnp.logical_and(wok[i], same[j])
 
     c_e = [
-        remote(pb.at[1, 2], pb.at[2, 2], E0, (w - 1, n)),
-        remote(pb.at[1, 2], pb.at[0, 2], E0 + 1, (w + 1, n)),
-    ]
-    for k in range(2):
-        when(jnp.logical_and(upper, d_send[k]), c_e[k].start)
+        remote(pb.at[1, 1:4], pb.at[2, 1:4], E0, (w - 1, n)),
+        remote(pb.at[1, 1:4], pb.at[0, 1:4], E0 + 1, (w + 1, n)),
+    ]
     c_p = []
     for k, (i, j) in enumerate(near):
+        src, dst = ((slice(1, 2), slice(3, 4)), (slice(1, 3), slice(1, 3)), (slice(2, 3), slice(0, 1)))[j]
         c_p.append(
-            remote(pb.at[1, 1], pb.at[2 - i, 2 - j], P0 + k, (w + side(i), n + side(j)))
+            remote(pb.at[1, src], pb.at[2 - i, dst], P0 + k, (w + side(i), n + side(j)))
         )
-        when(beside(i, j), c_p[k].start)
+
+    def plain(i, j):
+        return jnp.logical_and(beside(i, j), jnp.logical_not(upper)) if j == 1 else beside(i, j)
+
+    for k in range(2):
+        when(jnp.logical_and(upper, d_send[k]), c_e[k].start)
+    for k, (i, j) in enumerate(near):
+        when(plain(i, j), c_p[k].start)
 
     if SPREAD == 2:
         spread()
@@ -384,7 +402,7 @@
         c_wc[k].start()
 
     for k, (i, j) in enumerate(near):
-        when(beside(2 - i, 2 - j), c_p[k].wait_recv)
+        when(plain(2 - i, 2 - j), c_p[k].wait_recv)
 
     low = lane < 64
 
@@ -393,49 +411,48 @@
         for k in range(2):
             when(d_recv[k], c_e[k].wait_recv)
 
-    def coarse_stack(left_of, mid_of, right_of, dst):
+    def coarse_stack(first_row, taps, dst):
         def level(a, carry):
-            left = left_of(a).astype(F32)
-            mid = mid_of(a).astype(F32)
-            right = right_of(a).astype(F32)
-            tops = (
-                pltpu.roll(jnp.where(low, mid, left), 64, 1),
-                mid,
-                pltpu.roll(jnp.where(low, right, mid), 64, 1),
-            )
-            for b, t in enumerate(tops):
-                for e, v in enumerate(shifted(t, 64)):
-                    dst[pl.ds(pl.multiple_of(a * 1152 + (b * 3 + e) * 128, 128), 128), :] = v
+            q = [pb[a, first_row + r].astype(F32) if first_row + r < 4 else jnp.zeros((64, 128), F32) for r in range(taps + 1)]
+            z = [pltpu.roll(v, 64, 1) for v in q]
+            for b in range(taps):
+                for c in range(2):
+                    t = jnp.where(low, q[b], z[b + 1]) if c == 0 else jnp.where(low, z[b], q[b + 1])
+                    for e, v in enumerate(shifted(t, 64)):
+                        r0 = (b * 3 + e) * 128 + c * 64
+                        dst[pl.ds(pl.multiple_of(a * taps * 384 + r0, 64), 64), :] = v
             return carry
 
         lax.fori_loop(0, 3, level, 0)
 
-    coarse_stack(lambda a: pb[a, 0], lambda a: pb[a, 1], lambda a: pb[a, 2], xs3)
-    blank = jnp.zeros((128, 128), F32)
-    when(upper, lambda: coarse_stack(lambda a: pb[a, 1], lambda a: pb[a, 2], lambda a: blank, xs4))
+    coarse_stack(0, 3, xs3)
+    when(upper, lambda: coarse_stack(2, 2, xs4))
 
     for c in c_wc:
         c.wait_recv()
 
-    def coarse(src, whole):
-        def part(g, carry):
-            rows = pl.ds(pl.multiple_of(g * 128, 128), 128)
-            y = jnp.dot(w3g[rows, :], src[...], preferred_element_type=F32)
-            if whole:
-                ob[rows, :] = jnp.maximum(y, 0.0).astype(BF)
-            else:
-                of[rows, :] = y
-            return carry
-
-        lax.fori_loop(0, 2, part, 0)
-
-    when(jnp.logical_not(lower), lambda: coarse(xs3, True))
-    when(lower, lambda: coarse(xs3, False))
-    when(upper, lambda: coarse(xs4, False))
-
-    @pl.when(early)
-    def _():
-        pl.semaphore_wait(fsem.at[1], half)
+    def coarse(g):
+        rows = slice(g * 128, (g + 1) * 128)
+        y = jnp.dot(w3g[rows, :], xs3[...], preferred_element_type=F32)
+
+        @pl.when(lower)
+        def _():
+            of[rows, :] = y
+
+        @pl.when(jnp.logical_not(lower))
+        def _():
+            ob[rows, :] = jnp.maximum(y, 0.0).astype(BF)
+
+        @pl.when(upper)
+        def _():
+            t = None
+            for a in range(3):
+                p = jnp.dot(
+                    w3g[rows, a * 1152:a * 1152 + 768], xs4[a * 768:(a + 1) * 768, :],
+                    preferred_element_type=F32,
+                )
+                t = p if t is None else t + p
+            of[rows, :] = t
 
     def block(m):
         return out_ref.at[:, pl.ds(pl.multiple_of(m * 128, 128), 128)]
@@ -443,16 +460,34 @@
     def piece(ref, m):
         return ref.at[pl.ds(pl.multiple_of(m * 16, 16), 16), :]
 
-    c_a, c_b = [], []
-    for k in range(1, nn):
-        m = (n + k) % nn
-        c_a.append(remote(piece(ob, m), block(n), A0 + k, (w, m)))
-        c_b.append([
-            remote(piece(of, m), px.at[q], B0 + k, (w, m), r=B0 + q) for q in range(2)
-        ])
-        when(jnp.logical_not(lower), c_a[-1].start)
-        when(upper, c_b[-1][0].start)
-        when(lower, c_b[-1][1].start)
+    def sends(m):
+        return (
+            remote(piece(ob, m), block(n), A0 + m, (w, m), r=A0 + n),
+            remote(piece(of, m), px.at[0], B0 + m, (w, m), r=B0),
+            remote(piece(of, m), px.at[1], B0 + m, (w, m), r=B0 + 1),
+        )
+
+    def drop(m):
+        a, b, c = sends(m)
+        when(jnp.logical_not(lower), a.wait_send)
+        when(upper, b.wait_send)
+        when(lower, c.wait_send)
+
+    for g in range(2):
+        coarse(g)
+        if g == 0:
+            @pl.when(early)
+            def _():
+                pl.semaphore_wait(fsem.at[1], half)
+        for k in range(half):
+            m = g * half + k
+
+            @pl.when(m != n)
+            def _():
+                a, b, c = sends(m)
+                when(jnp.logical_not(lower), a.start)
+                when(upper, b.start)
+                when(lower, c.start)
 
     @pl.when(jnp.logical_not(lower))
     def _():
@@ -466,42 +501,37 @@
     def _():
         px[1] = of[mine, :]
 
-    for k in range(1, nn):
-        src = (n - k + nn) % nn
-        when(src != half, remote(piece(ob, n), block(src), A0 + k, (w, src)).wait_recv)
+    when(same[0], c_h[0].wait_send)
+    when(same[2], c_h[1].wait_send)
+    for k in range(2):
+        when(d_send[k], c_d[k].wait_send)
+    for k in range(2):
+        when(jnp.logical_and(outer, d_send[k]), c_g[k].wait_send)
+        when(d_recv[k], c_i[k].wait_send)
+    for k, (i, j) in enumerate(near):
+        when(plain(i, j), c_p[k].wait_send)
+    for c in c_wz + c_wx + c_wf[0] + c_wf[1] + c_wc:
+        c.wait_send()
+
+    @pl.when(lower)
+    def _():
+        c_x[0].wait_send()
+
+    @pl.when(upper)
+    def _():
+        for k in range(2):
+            when(d_send[k], c_x[1 + k].wait_send)
+            when(d_send[k], c_e[k].wait_send)
+
+    for m in range(nn):
+        if m != half:
+            when(m != n, remote(piece(ob, n), block(m), A0 + m, (w, m)).wait_recv)
     for q, home in enumerate((upper, lower)):
         when(jnp.logical_not(home), remote(piece(of, n), px.at[q], B0 + q, (w, half - 1 + q)).wait_recv)
     out_ref[:, half * 128:(half + 1) * 128] = jnp.maximum(px[0] + px[1], 0.0).astype(BF)
 
-    when(same[0], c_h[0].wait_send)
-    when(same[2], c_h[1].wait_send)
-    for k in range(2):
-        when(d_send[k], c_d[k].wait_send)
-    for k in range(4):
-        when(g_send[k], c_g[k].wait_send)
-    for k, (i, j) in enumerate(near):
-        when(beside(i, j), c_p[k].wait_send)
-    for c in c_wz + c_wx + c_wf[0] + c_wf[1] + c_wc:
-        c.wait_send()
-
-    @pl.when(lower)
-    def _():
-        c_x[0].wait_send()
-        for c in c_b:
-            c[1].wait_send()
-
-    @pl.when(upper)
-    def _():
-        for k in range(2):
-            when(d_send[k], c_x[1 + k].wait_send)
-            when(d_send[k], c_e[k].wait_send)
-        for c in c_b:
-            c[0].wait_send()
-
-    @pl.when(jnp.logical_not(lower))
-    def _():
-        for c in c_a:
-            c.wait_send()
+    for m in range(nn):
+        when(m != n, functools.partial(drop, m))
 
 
 def solution(mesh):
@@ -526,12 +556,12 @@
                 pltpu.VMEM((4 * 192, 1024), BF),
                 pltpu.VMEM((192, 576), BF),
                 pltpu.VMEM((384, 576), BF),
-                pltpu.VMEM((3, 3, 128, 128), BF),
+                pltpu.VMEM((3, 4, 64, 128), BF),
                 pltpu.VMEM((3456, 128), BF),
                 pltpu.VMEM((nn * 16, 3456), BF),
                 pltpu.VMEM((256, 128), BF),
                 pltpu.VMEM((128, 128), BF),
-                pltpu.VMEM((3456, 128), BF),
+                pltpu.VMEM((2304, 128), BF),
                 pltpu.VMEM((256, 128), F32),
                 pltpu.VMEM((2, 16, 128), F32),
                 pltpu.SemaphoreType.DMA((NSEM,)),

time: 42.2 us -> 39.8 us (0.943)
  Pallas kernels: 41.4 us -> 39 us
    pallas_call x1, Pallas kernels: 41.4 us -> 39 us  [body(): pl.pallas_call(functools.partial(kernel, nw, nn), out_shape=pltpu.VMEM((1...]
where the time goes in v4:
time: 39.8 us; the launch traced here: 39.6 us
  Pallas kernels  39 us (98%)
  local copies, waits for them, and re-layouts  0.63 us (2%)
    pallas_call x1, Pallas kernels, body(): pl.pallas_call(functools.partial(kernel, nw, nn), out_shape=pltpu.VMEM((1...  39 us

profile of v4, /device:TPU:129, one launch (start us, length us, event | category | flops | bytes accessed | tf_op | source)
XLA Modules:
  0.0 39.6 jit_solution(1900867800087166657)
XLA Ops:
  0.0 39.0 %shard_map.64 = bf16[16,2048]{1,0:T(8,128)(2,1)S(1)} custom-call(bf16[512,128]{1,0:T(8,128)(2,1)} %bitcast.7, f32[1,64]{1,0:T(1,128)} %bitcast.8, f32[1,64]{1,0:T(1,128)} %bitcast.9, bf16[64,1728]{1,0:T(8,128)(2,1)} %w1_hbm.1, bf16[1728,128]{1,0:T(8,128)(2,1)} %bitcast.6, bf16[16,3456]{1,0:T(8,128)(2,1)} %w3_hbm.1), custom_call_target="tpu_custom_call" | custom-call | tf_op jit(solution)/shard_map/pallas_call | solution.py:542
  39.0 0.6 %copy.8 = bf16[16,1,2048]{2,0,1:T(8,128)(2,1)} copy(bf16[16,1,2048]{2,0,1:T(8,128)(2,1)S(1)} %bitcast.5) | data formatting | bytes 131072

commit v5 on v4

--- a/solution.py
+++ b/solution.py
@@ -10,9 +10,8 @@
 BF = jnp.bfloat16
 F32 = jnp.float32
 MESH = pl.DeviceIdType.MESH
-SPREAD = 0
-
-names = dict(H=2, D=2, G=4, P=8, WX=3, WZ=2, WF=6, WC=8, A=16, X=3, E=2, B=16, L=6)
+
+names = dict(H=2, D=2, G=4, P=8, WX=3, WZ=2, WF=6, WC=8, A=1, X=6, E=2, B=3, L=6)
 BASE, NSEM = {}, 0
 for name, size in names.items():
     BASE[name] = NSEM
@@ -47,6 +46,16 @@
         return jnp.logical_and(wok[i], nok[j])
 
     near = [(i, j) for i in range(3) for j in range(3) if (i, j) != (1, 1)]
+
+    mine = pl.ds(pl.multiple_of(n * 16, 16), 16)
+    loads = [
+        pltpu.make_async_copy(src, dst, rsem.at[L0 + k])
+        for k, (src, dst) in enumerate((
+            (x_hbm, x_ref), (sc_hbm, sc_ref), (sh_hbm, sh_ref),
+            (w3_hbm, w3g.at[mine, :]), (w1_hbm, w1_ref), (w2_hbm, w2_ref),
+        ))
+    ]
+    loads[0].start()
 
     early = zh == 0
     late = zh == 1
@@ -82,15 +91,7 @@
     expected = half - 1 + wcount * (1 + count(same[0]) + count(same[2]))
     expected = expected + count(late) * (half + 1)
 
-    mine = pl.ds(pl.multiple_of(n * 16, 16), 16)
-    loads = [
-        pltpu.make_async_copy(src, dst, rsem.at[L0 + k])
-        for k, (src, dst) in enumerate((
-            (x_hbm, x_ref), (sc_hbm, sc_ref), (sh_hbm, sh_ref),
-            (w3_hbm, w3g.at[mine, :]), (w1_hbm, w1_ref), (w2_hbm, w2_ref),
-        ))
-    ]
-    for c in loads:
+    for c in loads[1:]:
         c.start()
 
     @pl.when(jnp.logical_or(n == 0, n == half))
@@ -186,9 +187,12 @@
     ]
     far = slice(768, 1280)
     c_x = [
-        remote(fb.at[2:4, :, own], fb.at[2:4, :, far], X0, (w, n - 1)),
-        remote(fb.at[2:4, :, far], fb.at[4:6, :, far], X0 + 1, (w - 1, n)),
-        remote(fb.at[2:4, :, far], fb.at[0:2, :, far], X0 + 2, (w + 1, n)),
+        [
+            remote(fb.at[2 + i:3 + i, :, own], fb.at[2 + i:3 + i, :, far], X0 + i, (w, n - 1)),
+            remote(fb.at[2 + i:3 + i, :, far], fb.at[4 + i:5 + i, :, far], X0 + 2 + i, (w - 1, n)),
+            remote(fb.at[2 + i:3 + i, :, far], fb.at[i:1 + i, :, far], X0 + 4 + i, (w + 1, n)),
+        ]
+        for i in range(2)
     ]
 
     def when(cond, f):
@@ -196,7 +200,8 @@
 
     upper = cross[2]
     lower = cross[0]
-    when(lower, c_x[0].start)
+    for i in range(2):
+        when(lower, c_x[i][0].start)
     when(same[0], c_h[0].start)
     when(same[2], c_h[1].start)
     for k in range(2):
@@ -333,11 +338,8 @@
 
     @pl.when(jnp.logical_not(upper))
     def _():
-        if SPREAD == 0:
-            spread()
+        when(late, spread)
         first(0, 6)
-        if SPREAD == 1:
-            spread()
         r0, r1 = second(0, 4)
         keep = jnp.where(lower, 0.0, 1.0)
         pb[1, 1] = (pack(r0) * keep).astype(BF)
@@ -345,20 +347,18 @@
 
     @pl.when(upper)
     def _():
-        c_x[0].wait_recv()
-        for k in range(2):
-            when(d_send[k], c_x[1 + k].start)
-        if SPREAD == 0:
-            spread()
+        for i in range(2):
+            c_x[i][0].wait_recv()
+            for k in range(2):
+                when(d_send[k], c_x[i][1 + k].start)
         for d in (2, 3):
             for h in range(6, 10):
                 stack1(d, h)
         first(0, 4)
-        if SPREAD == 1:
-            spread()
         rb[...] = second(0, 2)[0]
         for k in range(2):
-            when(d_recv[k], c_x[1 + k].wait_recv)
+            for i in range(2):
+                when(d_recv[k], c_x[i][1 + k].wait_recv)
         for d in (0, 1, 4, 5):
             for h in range(6, 10):
                 stack1(d, h)
@@ -394,13 +394,14 @@
     for k, (i, j) in enumerate(near):
         when(plain(i, j), c_p[k].start)
 
-    if SPREAD == 2:
-        spread()
-    for c in c_wf[0] + c_wf[1]:
-        c.wait_recv()
-    for k in range(5, 8):
-        c_wc[k].start()
-
+    def spread_rest():
+        for k in range(3):
+            for q in range(2):
+                c_wf[q][k].wait_recv()
+            c_wc[7 - k].start()
+
+    when(early, spread)
+    when(late, spread_rest)
     for k, (i, j) in enumerate(near):
         when(plain(2 - i, 2 - j), c_p[k].wait_recv)
 
@@ -428,8 +429,13 @@
     coarse_stack(0, 3, xs3)
     when(upper, lambda: coarse_stack(2, 2, xs4))
 
-    for c in c_wc:
+    for c in c_wc[:4]:
         c.wait_recv()
+
+    @pl.when(late)
+    def _():
+        for c in c_wc[4:]:
+            c.wait_recv()
 
     def coarse(g):
         rows = slice(g * 128, (g + 1) * 128)
@@ -462,32 +468,33 @@
 
     def sends(m):
         return (
-            remote(piece(ob, m), block(n), A0 + m, (w, m), r=A0 + n),
-            remote(piece(of, m), px.at[0], B0 + m, (w, m), r=B0),
-            remote(piece(of, m), px.at[1], B0 + m, (w, m), r=B0 + 1),
+            remote(piece(ob, m), block(n), A0, (w, m)),
+            remote(piece(of, m), px.at[0], B0 + 2, (w, m), r=B0),
+            remote(piece(of, m), px.at[1], B0 + 2, (w, m), r=B0 + 1),
         )
 
-    def drop(m):
-        a, b, c = sends(m)
-        when(jnp.logical_not(lower), a.wait_send)
-        when(upper, b.wait_send)
-        when(lower, c.wait_send)
-
     for g in range(2):
-        coarse(g)
-        if g == 0:
+        if g == 1:
             @pl.when(early)
             def _():
+                spread_rest()
+                for c in c_wc[4:]:
+                    c.wait_recv()
                 pl.semaphore_wait(fsem.at[1], half)
-        for k in range(half):
-            m = g * half + k
-
-            @pl.when(m != n)
+        coarse(g)
+        group = range(g * half, (g + 1) * half)
+
+        @pl.when(jnp.logical_not(lower))
+        def _():
+            for m in group:
+                when(m != n, sends(m)[0].start)
+
+        for q, home in enumerate((upper, lower)):
+            @pl.when(home)
             def _():
-                a, b, c = sends(m)
-                when(jnp.logical_not(lower), a.start)
-                when(upper, b.start)
-                when(lower, c.start)
+                for m in group:
+                    if m != half - 1 + q:
+                        sends(m)[1 + q].start()
 
     @pl.when(jnp.logical_not(lower))
     def _():
@@ -515,23 +522,28 @@
 
     @pl.when(lower)
     def _():
-        c_x[0].wait_send()
+        for i in range(2):
+            c_x[i][0].wait_send()
 
     @pl.when(upper)
     def _():
         for k in range(2):
-            when(d_send[k], c_x[1 + k].wait_send)
+            for i in range(2):
+                when(d_send[k], c_x[i][1 + k].wait_send)
             when(d_send[k], c_e[k].wait_send)
 
-    for m in range(nn):
-        if m != half:
-            when(m != n, remote(piece(ob, n), block(m), A0 + m, (w, m)).wait_recv)
+    def many(count):
+        return remote(ob.at[0:16 * count, :], ob.at[0:16 * count, :], A0, (w, mate))
+
+    when(lower, many(nn - 1).wait_recv)
+    when(jnp.logical_not(lower), many(nn - 2).wait_recv)
     for q, home in enumerate((upper, lower)):
         when(jnp.logical_not(home), remote(piece(of, n), px.at[q], B0 + q, (w, half - 1 + q)).wait_recv)
     out_ref[:, half * 128:(half + 1) * 128] = jnp.maximum(px[0] + px[1], 0.0).astype(BF)
 
-    for m in range(nn):
-        when(m != n, functools.partial(drop, m))
+    when(jnp.logical_not(lower), many(nn - 1).wait_send)
+    parts = of.at[0:16 * (nn - 1), :]
+    when(jnp.logical_or(upper, lower), remote(parts, parts, B0 + 2, (w, mate)).wait_send)
 
 
 def solution(mesh):

time: 39.8 us -> 39.5 us (level)
  the two profiles are of different devices: /device:TPU:129 before, /device:TPU:127 now
where the time goes in v5:
time: 39.5 us; the launch traced here: 39.4 us
  Pallas kernels  38.7 us (98%)
  local copies, waits for them, and re-layouts  0.63 us (2%)
    pallas_call x1, Pallas kernels, body(): pl.pallas_call(functools.partial(kernel, nw, nn), out_shape=pltpu.VMEM((1...  38.7 us

profile of v5, /device:TPU:127, one launch (start us, length us, event | category | flops | bytes accessed | tf_op | source)
XLA Modules:
  0.0 39.4 jit_solution(10296424616056099516)
XLA Ops:
  0.0 38.7 %shard_map.64 = bf16[16,2048]{1,0:T(8,128)(2,1)S(1)} custom-call(bf16[512,128]{1,0:T(8,128)(2,1)} %bitcast.7, f32[1,64]{1,0:T(1,128)} %bitcast.8, f32[1,64]{1,0:T(1,128)} %bitcast.9, bf16[64,1728]{1,0:T(8,128)(2,1)} %w1_hbm.1, bf16[1728,128]{1,0:T(8,128)(2,1)} %bitcast.6, bf16[16,3456]{1,0:T(8,128)(2,1)} %w3_hbm.1), custom_call_target="tpu_custom_call" | custom-call | tf_op jit(solution)/shard_map/pallas_call | solution.py:554
  38.7 0.6 %copy.8 = bf16[16,1,2048]{2,0,1:T(8,128)(2,1)} copy(bf16[16,1,2048]{2,0,1:T(8,128)(2,1)S(1)} %bitcast.5) | data formatting | bytes 131072

commit v6 on v5

--- a/solution.py
+++ b/solution.py
@@ -20,7 +20,7 @@
 
 
 def kernel(nw, nn, x_hbm, sc_hbm, sh_hbm, w1_hbm, w2_hbm, w3_hbm, out_ref,
-           x_ref, sc_ref, sh_ref, w1_ref, w2_ref, xf, fb, xs1, xs2, w1p, w2p, pb, xs3, w3g, ob, rb, xs4, of, px, ssem, rsem, fsem):
+           x_ref, sc_ref, sh_ref, w1_ref, w2_ref, xf, fb, xs1, xs2, w1p, w2p, pb, xs3, w3g, ob, rb, of, px, ssem, rsem, fsem):
     w = lax.axis_index("wide")
     n = lax.axis_index("narrow")
     half = nn // 2
@@ -204,8 +204,10 @@
         when(lower, c_x[i][0].start)
     when(same[0], c_h[0].start)
     when(same[2], c_h[1].start)
-    for k in range(2):
-        when(d_send[k], c_d[k].start)
+    near_cut = n == half + 1
+    held = [jnp.logical_and(near_cut, w == nw // 4), jnp.logical_and(near_cut, w == 3 * nw // 4 - 1)]
+    for k in range(2):
+        when(jnp.logical_and(d_send[k], jnp.logical_not(held[k])), c_d[k].start)
 
     def shard(m):
         return w3g.at[pl.ds(pl.multiple_of(m * 16, 16), 16), :]
@@ -250,6 +252,8 @@
 
     for j in range(2):
         when(same[2 * j], c_h[1 - j].wait_recv)
+    for k in range(2):
+        when(jnp.logical_and(d_send[k], held[k]), c_d[k].start)
     for k in range(2):
         when(jnp.logical_and(outer, d_send[k]), c_g[k].start)
     @pl.when(early)
@@ -347,6 +351,8 @@
 
     @pl.when(upper)
     def _():
+        for a in range(3):
+            xs3[a * 1152 + 768:(a + 1) * 1152, 128:256] = jnp.zeros((384, 128), BF)
         for i in range(2):
             c_x[i][0].wait_recv()
             for k in range(2):
@@ -356,6 +362,7 @@
                 stack1(d, h)
         first(0, 4)
         rb[...] = second(0, 2)[0]
+        spread()
         for k in range(2):
             for i in range(2):
                 when(d_recv[k], c_x[i][1 + k].wait_recv)
@@ -400,7 +407,7 @@
                 c_wf[q][k].wait_recv()
             c_wc[7 - k].start()
 
-    when(early, spread)
+    when(jnp.logical_and(early, jnp.logical_not(upper)), spread)
     when(late, spread_rest)
     for k, (i, j) in enumerate(near):
         when(plain(2 - i, 2 - j), c_p[k].wait_recv)
@@ -412,7 +419,7 @@
         for k in range(2):
             when(d_recv[k], c_e[k].wait_recv)
 
-    def coarse_stack(first_row, taps, dst):
+    def coarse_stack(first_row, taps, dst, cols):
         def level(a, carry):
             q = [pb[a, first_row + r].astype(F32) if first_row + r < 4 else jnp.zeros((64, 128), F32) for r in range(taps + 1)]
             z = [pltpu.roll(v, 64, 1) for v in q]
@@ -421,13 +428,13 @@
                     t = jnp.where(low, q[b], z[b + 1]) if c == 0 else jnp.where(low, z[b], q[b + 1])
                     for e, v in enumerate(shifted(t, 64)):
                         r0 = (b * 3 + e) * 128 + c * 64
-                        dst[pl.ds(pl.multiple_of(a * taps * 384 + r0, 64), 64), :] = v
+                        dst[pl.ds(pl.multiple_of(a * 1152 + r0, 64), 64), cols] = v
             return carry
 
         lax.fori_loop(0, 3, level, 0)
 
-    coarse_stack(0, 3, xs3)
-    when(upper, lambda: coarse_stack(2, 2, xs4))
+    coarse_stack(0, 3, xs3, slice(0, 128))
+    when(upper, lambda: coarse_stack(2, 2, xs3, slice(128, 256)))
 
     for c in c_wc[:4]:
         c.wait_recv()
@@ -439,26 +446,24 @@
 
     def coarse(g):
         rows = slice(g * 128, (g + 1) * 128)
-        y = jnp.dot(w3g[rows, :], xs3[...], preferred_element_type=F32)
-
-        @pl.when(lower)
+
+        @pl.when(jnp.logical_not(upper))
         def _():
-            of[rows, :] = y
-
-        @pl.when(jnp.logical_not(lower))
-        def _():
-            ob[rows, :] = jnp.maximum(y, 0.0).astype(BF)
+            y = jnp.dot(w3g[rows, :], xs3[:, 0:128], preferred_element_type=F32)
+
+            @pl.when(lower)
+            def _():
+                of[rows, :] = y
+
+            @pl.when(jnp.logical_not(lower))
+            def _():
+                ob[rows, :] = jnp.maximum(y, 0.0).astype(BF)
 
         @pl.when(upper)
         def _():
-            t = None
-            for a in range(3):
-                p = jnp.dot(
-                    w3g[rows, a * 1152:a * 1152 + 768], xs4[a * 768:(a + 1) * 768, :],
-                    preferred_element_type=F32,
-                )
-                t = p if t is None else t + p
-            of[rows, :] = t
+            y = jnp.dot(w3g[rows, :], xs3[...], preferred_element_type=F32)
+            ob[rows, :] = jnp.maximum(y[:, 0:128], 0.0).astype(BF)
+            of[rows, :] = y[:, 128:256]
 
     def block(m):
         return out_ref.at[:, pl.ds(pl.multiple_of(m * 128, 128), 128)]
@@ -569,11 +574,10 @@
                 pltpu.VMEM((192, 576), BF),
                 pltpu.VMEM((384, 576), BF),
                 pltpu.VMEM((3, 4, 64, 128), BF),
-                pltpu.VMEM((3456, 128), BF),
+                pltpu.VMEM((3456, 256), BF),
                 pltpu.VMEM((nn * 16, 3456), BF),
                 pltpu.VMEM((256, 128), BF),
                 pltpu.VMEM((128, 128), BF),
-                pltpu.VMEM((2304, 128), BF),
                 pltpu.VMEM((256, 128), F32),
                 pltpu.VMEM((2, 16, 128), F32),
                 pltpu.SemaphoreType.DMA((NSEM,)),

time: 39.5 us -> 39.2 us (level)
  no operation moved by 1% of the time
where the time goes in v6:
time: 39.2 us; the launch traced here: 39 us
  Pallas kernels  38.4 us (98%)
  local copies, waits for them, and re-layouts  0.63 us (2%)
    pallas_call x1, Pallas kernels, body(): pl.pallas_call(functools.partial(kernel, nw, nn), out_shape=pltpu.VMEM((1...  38.4 us

profile of v6, /device:TPU:127, one launch (start us, length us, event | category | flops | bytes accessed | tf_op | source)
XLA Modules:
  0.0 39.0 jit_solution(15290654330799752995)
XLA Ops:
  0.0 38.4 %shard_map.64 = bf16[16,2048]{1,0:T(8,128)(2,1)S(1)} custom-call(bf16[512,128]{1,0:T(8,128)(2,1)} %bitcast.7, f32[1,64]{1,0:T(1,128)} %bitcast.8, f32[1,64]{1,0:T(1,128)} %bitcast.9, bf16[64,1728]{1,0:T(8,128)(2,1)} %w1_hbm.1, bf16[1728,128]{1,0:T(8,128)(2,1)} %bitcast.6, bf16[16,3456]{1,0:T(8,128)(2,1)} %w3_hbm.1), custom_call_target="tpu_custom_call" | custom-call | tf_op jit(solution)/shard_map/pallas_call | solution.py:559
  38.4 0.6 %copy.8 = bf16[16,1,2048]{2,0,1:T(8,128)(2,1)} copy(bf16[16,1,2048]{2,0,1:T(8,128)(2,1)S(1)} %bitcast.5) | data formatting | bytes 131072

commit v7 on v6

--- a/solution.py
+++ b/solution.py
@@ -353,6 +353,7 @@
     def _():
         for a in range(3):
             xs3[a * 1152 + 768:(a + 1) * 1152, 128:256] = jnp.zeros((384, 128), BF)
+        first(0, 4)
         for i in range(2):
             c_x[i][0].wait_recv()
             for k in range(2):
@@ -360,7 +361,6 @@
         for d in (2, 3):
             for h in range(6, 10):
                 stack1(d, h)
-        first(0, 4)
         rb[...] = second(0, 2)[0]
         spread()
         for k in range(2):

time: 39.2 us -> 39.2 us (level)
  no operation moved by 1% of the time
where the time goes in v7:
time: 39.2 us; the launch traced here: 39 us
  Pallas kernels  38.4 us (98%)
  local copies, waits for them, and re-layouts  0.63 us (2%)
    pallas_call x1, Pallas kernels, body(): pl.pallas_call(functools.partial(kernel, nw, nn), out_shape=pltpu.VMEM((1...  38.4 us

profile of v7, /device:TPU:127, one launch (start us, length us, event | category | flops | bytes accessed | tf_op | source)
XLA Modules:
  0.0 39.0 jit_solution(13419502914696784330)
XLA Ops:
  0.0 38.4 %shard_map.64 = bf16[16,2048]{1,0:T(8,128)(2,1)S(1)} custom-call(bf16[512,128]{1,0:T(8,128)(2,1)} %bitcast.7, f32[1,64]{1,0:T(1,128)} %bitcast.8, f32[1,64]{1,0:T(1,128)} %bitcast.9, bf16[64,1728]{1,0:T(8,128)(2,1)} %w1_hbm.1, bf16[1728,128]{1,0:T(8,128)(2,1)} %bitcast.6, bf16[16,3456]{1,0:T(8,128)(2,1)} %w3_hbm.1), custom_call_target="tpu_custom_call" | custom-call | tf_op jit(solution)/shard_map/pallas_call | solution.py:559
  38.4 0.6 %copy.8 = bf16[16,1,2048]{2,0,1:T(8,128)(2,1)} copy(bf16[16,1,2048]{2,0,1:T(8,128)(2,1)S(1)} %bitcast.5) | data formatting | bytes 131072
